TPU v7x, 32 devices: a whole 2x2x4 slice. The times are simulated.
32 devices in a mesh: pb: 2 (over x), ka: 16 (over z, y, core).
Axes of the slice: x: 2, y: 2, z: 4, core: 2. Of those that a mesh axis runs over, the one named last changes fastest.
Arguments:
- coupling: bfloat16 [2, 16, 32, 32, 384], P('pb', 'ka'), may hold values from -0.796875 to 0.796875
- phonon_occ: float32 [2, 16, 32, 12], P('pb', 'ka'), may hold values from 0.1 to 1
- band_window: int32 [2, 16, 32, 32], P('pb', 'ka'), may hold values 0 or 1
- pair_count: int32 [2, 16, 16], P('pb', 'ka'), may hold values from 0 to 2, as said below
- k_target: int32 [2, 16, 32], P('pb', 'ka'), may hold values from 0 to 127
- kq_source: int32 [2, 16, 32], P('pb', 'ka'), may hold values from 0 to 127
- velocity: float32 [3, 32, 2048], P(None, None, 'ka'), may hold values from -6 to 6
- lifetime: float32 [32, 2048], P(None, 'ka'), may hold values from 0.5 to 2
Outputs:
- deviation: float32 [3, 32, 2048], P(None, None, 'ka')
Inputs may be any that keep to these rules, and one draw needn't show every extreme that they name: pair_count[p, a, d] is the number of live tile slots among slots d * 2 to d * 2 + 1 of device (p, a); in every q-group p some owner d receives 2 live tiles from every source.
All inputs are finite; a program needn't handle non-finite values. No bound on the sum of `band_window` on one device may be relied on, other than what follows from the above.
Results may differ from a plain program's by a relative error of at most 0.012.
Values may be sent and summed in bfloat16 or wider, within the bound.
A program may use at most 64 MiB of HBM per device.

v0:
```python
import functools

import jax
import jax.numpy as jnp
from jax import lax
from jax.experimental import pallas as pl
from jax.experimental.pallas import tpu as pltpu
from jax.sharding import PartitionSpec as P

ITERS = 4
LANES = 128
UNROLLED = 16
F32 = jnp.float32
BF16 = jnp.bfloat16


def iota(shape, axis):
    return lax.broadcasted_iota(jnp.int32, shape, axis)


def mask(condition):
    return jnp.where(condition, 1.0, 0.0)


def dot(a, b, dims=((1,), (0,)), precision=None):
    return lax.dot_general(a, b, (dims, ((), ())), precision=precision, preferred_element_type=F32)


def column(row, wanted):
    rows, width = wanted.shape
    return jnp.sum(jnp.where(wanted, jnp.broadcast_to(row, (rows, width)), 0.0), axis=1, keepdims=True)


def each(count, act):
    if count <= 2 * UNROLLED:
        for distance in sorted(range(1, count), key=lambda d: -min(d, count - d)):
            act(distance)
    else:

        def body(distance, carry):
            act(distance)
            return carry

        lax.fori_loop(1, count, body, 0)


def kernel(
    n_pb, n_ka, directions,
    *refs,
):
    inputs, out_ref, held = refs[:8], refs[8], refs[9:17]
    weights, tables, send, recv, load_sem, send_sem, recv_sem, share_send, share_recv = refs[17:]
    coupling_ref, occ_ref, window_ref, count_ref, target_ref, source_ref, velocity_ref, lifetime_ref = held
    loads = [pltpu.make_async_copy(x, y, load_sem.at[i]) for i, (x, y) in enumerate(zip(inputs, held))]
    for load in loads:
        load.start()
    p, a = lax.axis_index("pb"), lax.axis_index("ka")
    me = p * n_ka + a
    devices = n_pb * n_ka
    tiles, bands = window_ref.shape
    slots = tiles // n_ka
    modes = occ_ref.shape[0]
    wide = bands * modes
    width = velocity_ref.shape[1]
    row = recv.shape[-1]
    used = directions * bands
    low = 256 // bands
    span = low * bands
    groups = tiles // low

    barrier = pltpu.get_barrier_semaphore()

    def peer(step):
        other = lax.rem(me + step, devices)
        return {"pb": other // n_ka, "ka": lax.rem(other, n_ka)}

    def greet(distance):
        pl.semaphore_signal(barrier, inc=1, device_id=peer(distance), device_id_type=pl.DeviceIdType.MESH)

    each(devices, greet)
    for load in loads[1:]:
        load.wait()

    eye = iota((tiles, tiles), 0) == iota((tiles, tiles), 1)
    owner = iota((tiles, n_ka), 0) // slots == iota((tiles, n_ka), 1)
    live = mask((iota((tiles, 1), 0) % slots).astype(F32) < column(count_ref[...].astype(F32), owner))
    source = column(source_ref[...].astype(F32), eye)
    target = column(target_ref[...].astype(F32), eye)
    target_lane = jnp.where(iota((tiles, row), 1) == used, target, 0.0)
    shown = window_ref[...].astype(F32) * live

    def tile_tables(shown, source):
        pick = mask(source == iota((tiles, width), 1).astype(F32)).astype(BF16)
        keep = jnp.concatenate([shown] * groups, axis=1)
        at = (tiles, groups * bands)
        keep = jnp.where(iota(at, 1) // bands == iota(at, 0) // low, keep, 0.0)
        return pick, jnp.concatenate([keep] * directions, axis=0)

    own = tile_tables(shown, source)
    tables[p] = jnp.concatenate(
        [shown, jnp.where(iota((tiles, LANES - bands), 1) == 0, source, 0.0)], axis=1
    ).astype(BF16)
    place = mask(
        (iota((tiles, directions * span), 1) % span) // bands == iota((tiles, directions * span), 0) % low
    )
    shape = (row, directions * span)
    spread = mask(
        ((iota(shape, 0) // bands) == (iota(shape, 1) // span)) & (iota(shape, 0) % bands == iota(shape, 1) % bands)
    ).astype(BF16)
    shape = (directions * groups * bands, row)
    fold = mask(
        ((iota(shape, 0) // (groups * bands)) == (iota(shape, 1) // bands))
        & (iota(shape, 0) % bands == iota(shape, 1) % bands)
    ).astype(BF16)

    pad = jnp.zeros((row - used, width), F32)
    velocity = jnp.concatenate([velocity_ref[...], pad], axis=0).T
    lifetime = jnp.concatenate([lifetime_ref[...]] * directions + [pad], axis=0).T

    shape = (modes, wide)
    occ = dot(
        occ_ref[:, 0, :], mask(iota(shape, 1) % modes == iota(shape, 0)), ((0,), (0,)), lax.Precision.HIGHEST
    )
    shape = (wide, LANES)
    start = (iota(shape, 1) % bands) * modes
    gather = mask((iota(shape, 0) >= start) & (iota(shape, 0) < start + modes)).astype(BF16)
    per = LANES // bands
    lane_block = iota((bands, LANES), 1) // bands
    loads[0].wait()
    weight = []
    for group in range(groups):
        halves = []
        for half in range(low // per):
            total = jnp.zeros((bands, LANES), F32)
            for inner in range(per):
                tile = group * low + half * per + inner
                value = coupling_ref[tile].astype(F32)
                value = (value * value * occ[tile : tile + 1, :]).astype(BF16)
                total = jnp.where(lane_block == inner, dot(value, gather), total)
            halves.append(total)
        weight.append(jnp.concatenate(halves, axis=1))
    weight = jnp.concatenate(weight, axis=0).astype(BF16)
    weights[p] = weight

    def share(distance, held, index):
        return pltpu.make_async_remote_copy(
            src_ref=held.at[p],
            dst_ref=held.at[p],
            send_sem=share_send.at[index],
            recv_sem=share_recv.at[index],
            device_id={"pb": lax.rem(p + distance, n_pb), "ka": a},
            device_id_type=pl.DeviceIdType.MESH,
        )

    def tile_terms(chosen, pick_keep_weight):
        keep, weight = pick_keep_weight
        chosen = (dot(chosen, spread) * place).astype(BF16)
        chosen = jnp.concatenate([chosen[:, i * span : (i + 1) * span] for i in range(directions)], axis=0)
        terms = (dot(chosen, weight, ((1,), (1,))) * keep).astype(BF16)
        terms = jnp.concatenate([terms[i * tiles : (i + 1) * tiles] for i in range(directions)], axis=1)
        return dot(terms, fold)

    deviation = lifetime * velocity

    terms = tile_terms(dot(own[0], deviation.astype(BF16)).astype(BF16), (own[1], weight)) + target_lane
    send[0, 0] = terms.astype(BF16).reshape(n_ka, slots, row)
    pl.semaphore_wait(barrier, devices - 1)

    def post_all(distance):
        to = peer(distance)
        pltpu.make_async_remote_copy(
            src_ref=send.at[0, 0, to["ka"]],
            dst_ref=recv.at[0, p, a],
            send_sem=send_sem.at[0],
            recv_sem=recv_sem.at[0],
            device_id=to,
            device_id_type=pl.DeviceIdType.MESH,
        ).start()

    each(devices, post_all)
    pltpu.make_async_copy(send.at[0, 0, a], recv.at[0, p, a], recv_sem.at[0]).start()
    for distance in range(1, n_pb):
        share(distance, tables, 0).start()
        share(distance, weights, 1).start()
    for index, held in enumerate((tables, weights)):
        part = held.at[pl.ds(0, n_pb - 1)]
        pltpu.make_async_copy(part, part, share_recv.at[index]).wait()
    picks, keeps = [], []
    for q in range(n_pb):
        table = tables[q].astype(F32)
        pick, keep = tile_tables(table[:, :bands], table[:, bands : bands + 1])
        picks.append(pick)
        keeps.append(keep)
    pick = jnp.concatenate(picks, axis=0)

    def receive(step):
        pltpu.make_async_copy(recv.at[step], recv.at[step], recv_sem.at[step]).wait()
        return recv[step].reshape(devices * slots, row)

    arrived = receive(0)
    shape = (devices * slots, width)
    scatter = mask(arrived[:, used : used + 1].astype(F32) == iota(shape, 1).astype(F32)).T.astype(BF16)
    deviation = lifetime * (velocity + dot(scatter, arrived))

    for step in range(1, ITERS):
        chosen = dot(pick, deviation.astype(BF16)).astype(BF16)
        for q in range(n_pb):
            terms = tile_terms(chosen[q * tiles : (q + 1) * tiles], (keeps[q], weights[q]))
            send[step, q] = terms.astype(BF16).reshape(n_ka, slots, row)

        def post(distance):
            other = lax.rem(a + distance, n_ka)
            pltpu.make_async_remote_copy(
                src_ref=send.at[step, :, other],
                dst_ref=recv.at[step, :, a],
                send_sem=send_sem.at[step],
                recv_sem=recv_sem.at[step],
                device_id={"pb": p, "ka": other},
                device_id_type=pl.DeviceIdType.MESH,
            ).start()

        each(n_ka, post)
        pltpu.make_async_copy(send.at[step, :, a], recv.at[step, :, a], recv_sem.at[step]).start()
        deviation = lifetime * (velocity + dot(scatter, receive(step)))
    out_ref[...] = deviation.T[:used]
    for step in range(ITERS):
        if step:
            pieces = [recv.at[step, :, pl.ds(0, n_ka - 1)]]
        else:
            pieces = [recv.at[0, pl.ds(0, n_pb - 1)]] if n_pb > 1 else []
            pieces = pieces + [recv.at[0, 0, pl.ds(0, n_ka - 1)]]
        for piece in pieces:
            pltpu.make_async_copy(piece, piece, send_sem.at[step]).wait()
    for index, held in enumerate((tables, weights)):
        part = held.at[pl.ds(0, n_pb - 1)]
        pltpu.make_async_copy(part, part, share_send.at[index]).wait()


def shards(n_pb, n_ka, coupling, phonon_occ, band_window, pair_count, k_target, kq_source, velocity, lifetime):
    tiles = coupling.shape[2]
    directions, bands, width = velocity.shape
    slots = tiles // n_ka
    low = 256 // bands
    row = -(-(directions * bands + 1) // LANES) * LANES
    vmem = pl.BlockSpec(memory_space=pltpu.VMEM)
    operands = (
        coupling[0, 0], jnp.transpose(phonon_occ[0], (2, 0, 1)), band_window[0, 0], pair_count[0], k_target[0],
        kq_source[0], velocity.reshape(directions * bands, width), lifetime,
    )
    out = pl.pallas_call(
        functools.partial(kernel, n_pb, n_ka, directions),
        out_shape=pltpu.VMEM((directions * bands, width), F32),
        in_specs=[pl.BlockSpec(memory_space=pl.ANY)] * len(operands),
        out_specs=vmem,
        scratch_shapes=[
            *[pltpu.VMEM(x.shape, x.dtype) for x in operands],
            pltpu.VMEM((n_pb, tiles // low * bands, low * bands), BF16),
            pltpu.VMEM((n_pb, tiles, LANES), BF16),
            pltpu.VMEM((ITERS, n_pb, n_ka, slots, row), BF16),
            pltpu.VMEM((ITERS, n_pb, n_ka, slots, row), BF16),
            pltpu.SemaphoreType.DMA((len(operands),)),
            pltpu.SemaphoreType.DMA((ITERS,)),
            pltpu.SemaphoreType.DMA((ITERS,)),
            pltpu.SemaphoreType.DMA((2,)),
            pltpu.SemaphoreType.DMA((2,)),
        ],
        compiler_params=pltpu.CompilerParams(collective_id=0, has_side_effects=True),
    )(*operands)
    return out.reshape(directions, bands, width)


def solution(mesh):
    placed = (
        P("pb", "ka", None, None, None),
        P("pb", "ka", None, None),
        P("pb", "ka", None, None),
        P("pb", "ka", None),
        P("pb", "ka", None),
        P("pb", "ka", None),
        P(None, None, "ka"),
        P(None, "ka"),
    )
    return jax.shard_map(
        functools.partial(shards, mesh.shape["pb"], mesh.shape["ka"]),
        mesh=mesh, in_specs=placed, out_specs=P(None, None, "ka"), check_vma=False,
    )
```

profile of v0, /device:TPU:0, one launch (start us, length us, event | category | flops | bytes accessed | tf_op | source)
XLA Modules:
  0.0 27.4 jit_solution(7192195512389073238)
XLA Ops:
  0.0 26.8 %shard_map.82 = f32[96,128]{1,0:T(8,128)S(1)} custom-call(bf16[32,32,384]{2,1,0:T(8,128)(2,1)} %bitcast.11, f32[12,1,32]{2,1,0:T(1,128)} %bitcast.14, s32[32,32]{1,0:T(8,128)} %bitcast.13, s32[1,16]{1,0:T(1,128)} %bitcast.15, s32[1,32]{1,0:T(1,128)} %bitcast.16, s32[1,32]{1,0:T(1,128)} %bitcast.17, f32[96,128]{1,0:T(8,128)} %bitcast.12, f32[32,128]{1,0:T(8,128)} %refs_7_.1), custom_call_target="tpu_custom_call" | custom-call | tf_op jit(solution)/shard_map/pallas_call | solution.py:250
  26.8 0.6 %copy.10 = f32[3,32,128]{2,1,0:T(8,128)} copy(f32[3,32,128]{2,1,0:T(8,128)S(1)} %bitcast.10) | data formatting | bytes 98304
where the time goes:
time: 27.6 us; the launch traced here: 27.4 us
  Pallas kernels  26.8 us (97%)
  local copies, waits for them, and re-layouts  0.62 us (2%)
    pallas_call x1, Pallas kernels, shards(): pl.pallas_call(functools.partial(kernel, n_pb, n_ka, directions), out_sha...  26.8 us
    unnamed x1, local copies, waits for them, and re-layouts  0.62 us

commit v1 on v0

--- a/solution.py
+++ b/solution.py
@@ -236,6 +236,375 @@
         pltpu.make_async_copy(part, part, share_send.at[index]).wait()
 
 
+SUBLANES = 8
+HALVES = 2
+
+
+def wrapped(at, count):
+    moved = [at]
+    for step in range(1, count):
+        other = at + step
+        moved.append(jnp.where(other >= count, other - count, other))
+    return moved
+
+
+def far_first(sizes):
+    steps = [()]
+    for size in sizes:
+        steps = [old + (d,) for old in steps for d in range(size)]
+    return sorted(steps, key=lambda step: -sum(min(d, n - d) for d, n in zip(step, sizes)))
+
+
+def fold_rows(parts):
+    row = iota(parts[0].shape, 0)
+
+    def meet(a, b, width):
+        first = (row % (2 * width)) < width
+        up = pltpu.roll(a, SUBLANES - width, axis=0)
+        down = pltpu.roll(b, width, axis=0)
+        return jnp.where(first, a, b) + jnp.where(first, up, down)
+
+    width = SUBLANES // 2
+    while width:
+        half = len(parts) // 2
+        parts = [meet(parts[j], parts[j + half], width) for j in range(half)]
+        width //= 2
+    return parts[0]
+
+
+def owner_kernel(
+    grid, directions,
+    *refs,
+):
+    inputs, out_ref, held = refs[:8], refs[8], refs[9:17]
+    (gather_ref, rows_ref, weight_ref, first_send, bulk_send, side_send, bulk_recv, side_recv, terms_send, recv, last_recv,
+     load_sem, bulk_sems, side_sems, send_sem, recv_sem) = refs[17:]
+    coupling_ref, occ_ref, window_ref, count_ref, target_ref, source_ref, velocity_ref, lifetime_ref = held
+    loads = [pltpu.make_async_copy(x, y, load_sem.at[i]) for i, (x, y) in enumerate(zip(inputs, held))]
+    for load in loads:
+        load.start()
+    nx, ny, nz, nc = grid
+    depth = nz // HALVES
+    n_ka = nz * ny * nc
+    devices = nx * n_ka
+    owners = nc * ny * HALVES
+    tiles, bands = window_ref.shape
+    slots = tiles // n_ka
+    modes = occ_ref.shape[0]
+    wide = bands * modes
+    width = velocity_ref.shape[1]
+    used = directions * bands
+    outer = bands // SUBLANES
+    groups = nx * depth
+
+    p, a = lax.axis_index("pb"), lax.axis_index("ka")
+    c = lax.rem(a, nc)
+    y = lax.rem(lax.div(a, nc), ny)
+    z = lax.div(a, nc * ny)
+    half = lax.div(z, depth)
+    level = lax.rem(z, depth)
+    is_owner = (c == nc - 1) & (z == half + (depth - 1))
+    mine = (p * ny + y) * HALVES + half
+    host = (c * ny + y) * HALVES + half
+    group = p * depth + level
+    at_x, at_y, at_z, at_c, at_half = wrapped(p, nx), wrapped(y, ny), wrapped(z, nz), wrapped(c, nc), wrapped(half, HALVES)
+    owner_steps = far_first((nx, ny, HALVES))
+    all_steps = far_first((nx, ny, nz, nc))
+
+    def owner_at(x, y, half):
+        return {"pb": x, "ka": ((half + (depth - 1)) * ny + y) * nc + (nc - 1)}
+
+    def device_at(x, y, z, c):
+        return {"pb": x, "ka": (z * ny + y) * nc + c}
+
+    barrier = pltpu.get_barrier_semaphore()
+
+    def greet(to):
+        pl.semaphore_signal(barrier, inc=1, device_id=to, device_id_type=pl.DeviceIdType.MESH)
+
+    @pl.when(is_owner)
+    def _():
+        for dx, dy, dz, dc in all_steps[:-1]:
+            greet(device_at(at_x[dx], at_y[dy], at_z[dz], at_c[dc]))
+
+    @pl.when(jnp.logical_not(is_owner))
+    def _():
+        for dx, dy, dh in owner_steps:
+            greet(owner_at(at_x[dx], at_y[dy], at_half[dh]))
+
+    def remote(src, dst, sent, came, to):
+        pltpu.make_async_remote_copy(
+            src_ref=src, dst_ref=dst, send_sem=sent, recv_sem=came,
+            device_id=to, device_id_type=pl.DeviceIdType.MESH,
+        ).start()
+
+    def await_bytes(ref, semaphore):
+        pltpu.make_async_copy(ref, ref, semaphore).wait()
+
+    shape = (outer * wide, LANES)
+    chunk = iota(shape, 0) - (iota(shape, 1) % bands) * modes - (iota(shape, 1) // bands) * wide
+    gather_ref[...] = mask((chunk >= 0) & (chunk < modes)).astype(BF16)
+    span = tiles * SUBLANES
+    shape = (directions * LANES, LANES)
+    reduce = mask(
+        (iota(shape, 1) // bands == iota(shape, 0) // LANES)
+        & (iota(shape, 1) % bands // SUBLANES == iota(shape, 0) % LANES // bands)
+    ).astype(BF16)
+
+    for load in loads[1:]:
+        load.wait()
+    eye = iota((tiles, tiles), 0) == iota((tiles, tiles), 1)
+    in_block = iota((tiles, n_ka), 0) // slots == iota((tiles, n_ka), 1)
+    live = mask((iota((tiles, 1), 0) % slots).astype(F32) < column(count_ref[...].astype(F32), in_block))
+    source_row = source_ref[...].astype(F32)
+    target_row = target_ref[...].astype(F32)
+    source = column(source_row, eye)
+    target = column(target_row, eye)
+    shown = window_ref[...].astype(F32) * live
+    velocity = velocity_ref[...]
+    lifetime = lifetime_ref[...]
+    long_lifetime = jnp.concatenate([lifetime] * directions, axis=0)
+
+    copies = mask(iota((span, tiles), 0) // SUBLANES == iota((span, tiles), 1)).astype(BF16)
+    shown = dot(copies, shown.astype(BF16))
+    shown = jnp.where(iota(shown.shape, 1) % SUBLANES == iota(shown.shape, 0) % SUBLANES, shown, 0.0).astype(BF16)
+    shown = dot(shown, mask(iota((bands, LANES), 0) // SUBLANES == iota((bands, LANES), 1) // bands).astype(BF16))
+
+    start = (long_lifetime * velocity).astype(BF16)
+    start = jnp.concatenate(
+        [start[i * bands : (i + 1) * bands] for i in range(directions) for _ in range(outer)], axis=0
+    )
+    long_source = column(source_row, iota((span, tiles), 0) // SUBLANES == iota((span, tiles), 1))
+    long_pick = mask(long_source == iota((span, width), 1).astype(F32)).astype(BF16)
+    start = dot(long_pick, start, ((1,), (1,)))
+
+    both = jnp.concatenate([velocity, lifetime], axis=0)
+    pieces = []
+    for _ in range(3):
+        pieces.append(both.astype(BF16))
+        both = both - pieces[-1].astype(F32)
+    pick = mask(source == iota((tiles, width), 1).astype(F32)).astype(BF16)
+    both = dot(pick, jnp.concatenate(pieces, axis=0), ((1,), (1,)))
+    side_send[:tiles] = both[:, 2 * LANES :] + both[:, LANES : 2 * LANES] + both[:, :LANES]
+    shape = (SUBLANES, LANES)
+    side_send[tiles:] = jnp.where(
+        (iota(shape, 0) == 0) & (iota(shape, 1) // tiles == group),
+        jnp.broadcast_to(jnp.concatenate([target_row] * groups, axis=1), shape), 0.0,
+    )
+    key = source + (level * width).astype(F32)
+    bulk_send[SUBLANES * tiles :] = jnp.broadcast_to(key, (tiles, LANES)).astype(BF16)
+
+    shape = (modes, wide)
+    occ = dot(
+        occ_ref[:, 0, :], mask(iota(shape, 1) % modes == iota(shape, 0)), ((0,), (0,)), lax.Precision.HIGHEST
+    )
+    loads[0].wait()
+    rows = [[] for _ in range(outer)]
+    for tile in range(tiles):
+        value = coupling_ref[tile].astype(F32)
+        value = value * value * occ[tile : tile + 1, :]
+        for at in range(outer):
+            rows[at].append(value[at * SUBLANES : (at + 1) * SUBLANES])
+    rows = jnp.concatenate([jnp.concatenate(part, axis=0).astype(BF16) for part in rows], axis=1)
+    weight = (dot(rows, gather_ref[...]) * shown).astype(BF16).astype(F32)
+    rows_ref[0] = weight
+    rows = jnp.concatenate(
+        [(weight * start[:, i * LANES : (i + 1) * LANES]).astype(BF16) for i in range(directions)], axis=1
+    )
+    rows_ref[1] = dot(rows, reduce)
+    lane = iota((tiles, LANES), 1)
+    terms = jnp.where(lane == used, target, 0.0)
+    for at in range(SUBLANES):
+        part = rows_ref[1, pl.ds(at, tiles, stride=SUBLANES), :]
+        terms = jnp.where((lane % SUBLANES == at) & (lane < used), part, terms)
+        bulk_send[at * tiles : (at + 1) * tiles] = rows_ref[0, pl.ds(at, tiles, stride=SUBLANES), :].astype(BF16)
+    first_send[...] = terms.astype(BF16).reshape(first_send.shape)
+
+    @pl.when(is_owner)
+    def _():
+        pl.semaphore_wait(barrier, devices - 1)
+
+    @pl.when(jnp.logical_not(is_owner))
+    def _():
+        pl.semaphore_wait(barrier, owners)
+
+    def local_or_remote(local, src, dst, sent, came, to):
+        @pl.when(local)
+        def _():
+            pltpu.make_async_copy(src, dst, came).start()
+
+        @pl.when(jnp.logical_not(local))
+        def _():
+            remote(src, dst, sent, came, to)
+
+    for dx, dy, dh in owner_steps:
+        x, yy, hh = at_x[dx], at_y[dy], at_half[dh]
+        args = (first_send.at[hh, :, yy, x], recv.at[0, host, p, level], send_sem.at[0], recv_sem.at[0], owner_at(x, yy, hh))
+        if dx or dy or dh:
+            remote(*args)
+        else:
+            local_or_remote(is_owner, *args)
+    keeper = owner_at(c, y, half)
+    stays = is_owner & (c == p)
+    local_or_remote(stays, side_send, side_recv.at[group], side_sems.at[0], side_sems.at[1], keeper)
+    local_or_remote(stays, bulk_send, bulk_recv.at[group], bulk_sems.at[0], bulk_sems.at[1], keeper)
+
+    @pl.when(is_owner)
+    def _():
+        await_bytes(side_recv, side_sems.at[1])
+        both = side_recv[:, :tiles].reshape(LANES, LANES).T
+        velocity = both[:used]
+        lifetime = jnp.concatenate([both[used:]] * directions, axis=0)
+        target_rows = side_recv[0, tiles:]
+        for at in range(1, groups):
+            target_rows = target_rows + side_recv[at, tiles:]
+        tail = jnp.concatenate([target_rows, jnp.zeros((LANES - used - SUBLANES, LANES), F32)], axis=0)
+        choose = None
+        for step in range(1, ITERS):
+            await_bytes(recv.at[step - 1], recv_sem.at[step - 1])
+            arrived = recv[step - 1].reshape(LANES, LANES).T
+            if step == 1:
+                row_key = arrived[used : used + 1].astype(F32)
+                row_key = row_key + (iota((1, LANES), 1) // slots % depth * width).astype(F32)
+                await_bytes(bulk_recv, bulk_sems.at[1])
+                key = bulk_recv[:, SUBLANES * tiles :].reshape(LANES, LANES).astype(F32)
+                choose = mask(key == row_key).astype(BF16)
+            value = lifetime * (velocity + dot(arrived[:used], choose, ((1,), (1,))))
+            value = value.astype(BF16).astype(F32)
+            if step == 1:
+                for at in range(SUBLANES):
+                    part = bulk_recv[:, at * tiles : (at + 1) * tiles].reshape(LANES, LANES).T
+                    weight_ref[at * LANES : (at + 1) * LANES] = part.astype(F32)
+            terms = [[] for _ in range(directions)]
+            for at in range(outer):
+                parts = [[] for _ in range(directions)]
+                for inner in range(SUBLANES):
+                    totals = [None] * directions
+                    for m in range(0, bands, SUBLANES):
+                        first = inner * LANES + at * bands + m
+                        factor = weight_ref[first : first + SUBLANES]
+                        for i in range(directions):
+                            term = factor * value[i * bands + m : i * bands + m + SUBLANES]
+                            totals[i] = term if totals[i] is None else totals[i] + term
+                    for i in range(directions):
+                        parts[i].append(totals[i])
+                for i in range(directions):
+                    terms[i].append(fold_rows(parts[i]))
+            terms = jnp.concatenate([part for found in terms for part in found] + [tail], axis=0)
+            terms_send[step - 1] = terms.astype(BF16).T.reshape(terms_send.shape[1:])
+            if step < ITERS - 1:
+                for dx, dy, dh in owner_steps:
+                    x, yy, hh = at_x[dx], at_y[dy], at_half[dh]
+                    src, dst = terms_send.at[step - 1, :, hh, :, yy, x], recv.at[step, mine].reshape(groups, depth, slots, LANES)
+                    if dx or dy or dh:
+                        remote(src, dst, send_sem.at[step], recv_sem.at[step], owner_at(x, yy, hh))
+                    else:
+                        pltpu.make_async_copy(src, dst, recv_sem.at[step]).start()
+            else:
+                for dx, dy, dz, dc in all_steps:
+                    x, yy, zz, cc = at_x[dx], at_y[dy], at_z[dz], at_c[dc]
+                    src = terms_send.at[step - 1, :, lax.div(zz, depth), lax.rem(zz, depth), yy, cc]
+                    dst = last_recv.at[mine]
+                    if dx or dy or dz or dc:
+                        remote(src, dst, send_sem.at[step], recv_sem.at[step], device_at(x, yy, zz, cc))
+                    else:
+                        pltpu.make_async_copy(src, dst, recv_sem.at[step]).start()
+
+    await_bytes(last_recv, recv_sem.at[ITERS - 1])
+    arrived = last_recv[...].reshape(devices * slots, LANES).T
+    scatter = mask(
+        arrived[used : used + 1].astype(F32) == iota((width, devices * slots), 0).astype(F32)
+    ).astype(BF16)
+    out_ref[...] = long_lifetime * (velocity + dot(arrived[:used], scatter, ((1,), (1,))))
+
+    @pl.when(is_owner)
+    def _():
+        await_bytes(recv.at[0, pl.ds(0, owners - 1), 0, 0], send_sem.at[0])
+        for step in range(1, ITERS - 1):
+            await_bytes(recv.at[step, pl.ds(0, owners - 1)], send_sem.at[step])
+        for _ in range(groups - 1):
+            await_bytes(last_recv, send_sem.at[ITERS - 1])
+        await_bytes(last_recv.at[pl.ds(0, owners - 1)], send_sem.at[ITERS - 1])
+
+    @pl.when(jnp.logical_not(is_owner))
+    def _():
+        await_bytes(recv.at[0, :, 0, 0], send_sem.at[0])
+
+    @pl.when(jnp.logical_not(stays))
+    def _():
+        await_bytes(side_send, side_sems.at[0])
+        await_bytes(bulk_send, bulk_sems.at[0])
+
+
+def chip_grid(mesh):
+    spots = [[(*getattr(d, "coords", ()), getattr(d, "core_on_chip", None)) for d in row] for row in mesh.devices]
+    flat = [spot for row in spots for spot in row]
+    if any(len(spot) != 4 or None in spot for spot in flat):
+        return None
+    sizes = tuple(len({spot[i] for spot in flat}) for i in range(4))
+    nx, ny, nz, nc = sizes
+    low = [min(spot[i] for spot in flat) for i in range(4)]
+    for p, row in enumerate(spots):
+        for a, spot in enumerate(row):
+            if tuple(s - l for s, l in zip(spot, low)) != (p, a // nc % ny, a // (nc * ny), a % nc):
+                return None
+    return sizes if nx == nc and nz % HALVES == 0 else None
+
+
+def fits(grid, coupling, velocity):
+    if grid is None:
+        return False
+    nx, ny, nz, nc = grid
+    tiles = coupling.shape[2]
+    directions, bands, width = velocity.shape
+    depth = nz // HALVES
+    return (
+        nx * depth * tiles == LANES and bands * bands == SUBLANES * LANES and (directions + 1) * bands == LANES
+        and depth * width <= 256 and width == LANES
+    )
+
+
+def owner_shards(grid, coupling, phonon_occ, band_window, pair_count, k_target, kq_source, velocity, lifetime):
+    nx, ny, nz, nc = grid
+    tiles = coupling.shape[2]
+    directions, bands, width = velocity.shape
+    slots = tiles // (nz * ny * nc)
+    depth = nz // HALVES
+    groups = nx * depth
+    owners = nc * ny * HALVES
+    operands = (
+        coupling[0, 0], jnp.transpose(phonon_occ[0], (2, 0, 1)), band_window[0, 0], pair_count[0], k_target[0],
+        kq_source[0], velocity.reshape(directions * bands, width), lifetime,
+    )
+    out = pl.pallas_call(
+        functools.partial(owner_kernel, grid, directions),
+        out_shape=pltpu.VMEM((directions * bands, width), F32),
+        in_specs=[pl.BlockSpec(memory_space=pl.ANY)] * len(operands),
+        out_specs=pl.BlockSpec(memory_space=pltpu.VMEM),
+        scratch_shapes=[
+            *[pltpu.VMEM(x.shape, x.dtype) for x in operands],
+            pltpu.VMEM((bands // SUBLANES * coupling.shape[-1], LANES), BF16),
+            pltpu.VMEM((2, tiles * SUBLANES, LANES), F32),
+            pltpu.VMEM((SUBLANES * LANES, LANES), F32),
+            pltpu.VMEM((HALVES, depth, ny, nc, slots, LANES), BF16),
+            pltpu.VMEM(((SUBLANES + 1) * tiles, LANES), BF16),
+            pltpu.VMEM((tiles + SUBLANES, LANES), F32),
+            pltpu.VMEM((groups, (SUBLANES + 1) * tiles, LANES), BF16),
+            pltpu.VMEM((groups, tiles + SUBLANES, LANES), F32),
+            pltpu.VMEM((ITERS - 1, groups, HALVES, depth, ny, nc, slots, LANES), BF16),
+            pltpu.VMEM((ITERS - 1, owners, nx, depth, depth, slots, LANES), BF16),
+            pltpu.VMEM((owners, groups, slots, LANES), BF16),
+            pltpu.SemaphoreType.DMA((len(operands),)),
+            pltpu.SemaphoreType.DMA((2,)),
+            pltpu.SemaphoreType.DMA((2,)),
+            pltpu.SemaphoreType.DMA((ITERS,)),
+            pltpu.SemaphoreType.DMA((ITERS,)),
+        ],
+        compiler_params=pltpu.CompilerParams(collective_id=0, has_side_effects=True),
+    )(*operands)
+    return out.reshape(directions, bands, width)
+
+
 def shards(n_pb, n_ka, coupling, phonon_occ, band_window, pair_count, k_target, kq_source, velocity, lifetime):
     tiles = coupling.shape[2]
     directions, bands, width = velocity.shape
@@ -280,7 +649,14 @@
         P(None, None, "ka"),
         P(None, "ka"),
     )
+    grid = chip_grid(mesh)
+
+    def step(*args):
+        if fits(grid, args[0], args[6]):
+            return owner_shards(grid, *args)
+        return shards(mesh.shape["pb"], mesh.shape["ka"], *args)
+
     return jax.shard_map(
-        functools.partial(shards, mesh.shape["pb"], mesh.shape["ka"]),
+        step,
         mesh=mesh, in_specs=placed, out_specs=P(None, None, "ka"), check_vma=False,
     )

time: 27.6 us -> 20.9 us (0.76)
  Pallas kernels: 26.8 us -> 20.2 us
    pallas_call x1, Pallas kernels: 26.8 us -> 20.2 us  [owner_shards(): pl.pallas_call(functools.partial(owner_kernel, grid, directions), out_sha...]
where the time goes in v1:
time: 20.9 us; the launch traced here: 20.8 us
  Pallas kernels  20.2 us (97%)
  local copies, waits for them, and re-layouts  0.62 us (3%)
    pallas_call x1, Pallas kernels, owner_shards(): pl.pallas_call(functools.partial(owner_kernel, grid, directions), out_sha...  20.2 us
    unnamed x1, local copies, waits for them, and re-layouts  0.62 us

profile of v1, /device:TPU:0, one launch (start us, length us, event | category | flops | bytes accessed | tf_op | source)
XLA Modules:
  0.0 20.8 jit_solution(9998560466178300358)
XLA Ops:
  0.0 20.2 %shard_map.82 = f32[96,128]{1,0:T(8,128)S(1)} custom-call(bf16[32,32,384]{2,1,0:T(8,128)(2,1)} %bitcast.11, f32[12,1,32]{2,1,0:T(1,128)} %bitcast.14, s32[32,32]{1,0:T(8,128)} %bitcast.13, s32[1,16]{1,0:T(1,128)} %bitcast.15, s32[1,32]{1,0:T(1,128)} %bitcast.16, s32[1,32]{1,0:T(1,128)} %bitcast.17, f32[96,128]{1,0:T(8,128)} %bitcast.12, f32[32,128]{1,0:T(8,128)} %refs_7_.1), custom_call_target="tpu_custom_call" | custom-call | tf_op jit(solution)/shard_map/pallas_call | solution.py:579
  20.2 0.6 %copy.10 = f32[3,32,128]{2,1,0:T(8,128)} copy(f32[3,32,128]{2,1,0:T(8,128)S(1)} %bitcast.10) | data formatting | bytes 98304

commit v2 on v1

--- a/solution.py
+++ b/solution.py
@@ -260,6 +260,8 @@
 
     def meet(a, b, width):
         first = (row % (2 * width)) < width
+        if 2 * width == SUBLANES:
+            return jnp.where(first, a, b) + pltpu.roll(jnp.where(first, b, a), width, axis=0)
         up = pltpu.roll(a, SUBLANES - width, axis=0)
         down = pltpu.roll(b, width, axis=0)
         return jnp.where(first, a, b) + jnp.where(first, up, down)
@@ -277,10 +279,11 @@
     *refs,
 ):
     inputs, out_ref, held = refs[:8], refs[8], refs[9:17]
-    (gather_ref, rows_ref, weight_ref, first_send, bulk_send, side_send, bulk_recv, side_recv, terms_send, recv, last_recv,
+    (gather_ref, rows_ref, weight_ref, first_send, bulk_send, side_send, bulk_recv, side_recv, terms_send, recv, last_send, last_recv,
      load_sem, bulk_sems, side_sems, send_sem, recv_sem) = refs[17:]
     coupling_ref, occ_ref, window_ref, count_ref, target_ref, source_ref, velocity_ref, lifetime_ref = held
-    loads = [pltpu.make_async_copy(x, y, load_sem.at[i]) for i, (x, y) in enumerate(zip(inputs, held))]
+    loads = [pltpu.make_async_copy(x, y, load_sem.at[i]) for i, (x, y) in enumerate(zip(inputs[1:], held[1:]))]
+    loads.append(pltpu.make_async_copy(inputs[0], coupling_ref, load_sem.at[len(loads)]))
     for load in loads:
         load.start()
     nx, ny, nz, nc = grid
@@ -304,12 +307,16 @@
     half = lax.div(z, depth)
     level = lax.rem(z, depth)
     is_owner = (c == nc - 1) & (z == half + (depth - 1))
+    is_other = jnp.logical_not(is_owner)
     mine = (p * ny + y) * HALVES + half
     host = (c * ny + y) * HALVES + half
     group = p * depth + level
-    at_x, at_y, at_z, at_c, at_half = wrapped(p, nx), wrapped(y, ny), wrapped(z, nz), wrapped(c, nc), wrapped(half, HALVES)
+    at_x, at_y, at_half = wrapped(p, nx), wrapped(y, ny), wrapped(half, HALVES)
     owner_steps = far_first((nx, ny, HALVES))
-    all_steps = far_first((nx, ny, nz, nc))
+    owner_list = [(x, yy, hh) for x in range(nx) for yy in range(ny) for hh in range(HALVES)]
+    owner_list = [spot for pair in zip(owner_list, owner_list[::-1]) for spot in pair][: len(owner_list)]
+    every = [(x, yy, zz, cc) for zz in range(nz) for yy in range(ny) for x in range(nx) for cc in range(nc)]
+    every = sorted(every, key=lambda spot: sum(spot[:3]))
 
     def owner_at(x, y, half):
         return {"pb": x, "ka": ((half + (depth - 1)) * ny + y) * nc + (nc - 1)}
@@ -322,21 +329,38 @@
     def greet(to):
         pl.semaphore_signal(barrier, inc=1, device_id=to, device_id_type=pl.DeviceIdType.MESH)
 
+    def per_device(act):
+        for x, yy, zz, cc in every:
+            hh = zz // depth
+            if cc == nc - 1 and zz == hh + depth - 1:
+                there = (x * ny + yy) * HALVES + hh
+                pl.when(mine == there)(functools.partial(act, (x, yy, zz, cc), True))
+                pl.when(mine != there)(functools.partial(act, (x, yy, zz, cc), False))
+            else:
+                act((x, yy, zz, cc), False)
+
     @pl.when(is_owner)
     def _():
-        for dx, dy, dz, dc in all_steps[:-1]:
-            greet(device_at(at_x[dx], at_y[dy], at_z[dz], at_c[dc]))
-
-    @pl.when(jnp.logical_not(is_owner))
-    def _():
-        for dx, dy, dh in owner_steps:
-            greet(owner_at(at_x[dx], at_y[dy], at_half[dh]))
+        def act(spot, is_here):
+            if not is_here:
+                greet(device_at(*spot))
+
+        per_device(act)
 
     def remote(src, dst, sent, came, to):
         pltpu.make_async_remote_copy(
             src_ref=src, dst_ref=dst, send_sem=sent, recv_sem=came,
             device_id=to, device_id_type=pl.DeviceIdType.MESH,
         ).start()
+
+    def local_or_remote(local, src, dst, sent, came, to):
+        @pl.when(local)
+        def _():
+            pltpu.make_async_copy(src, dst, came).start()
+
+        @pl.when(jnp.logical_not(local))
+        def _():
+            remote(src, dst, sent, came, to)
 
     def await_bytes(ref, semaphore):
         pltpu.make_async_copy(ref, ref, semaphore).wait()
@@ -351,54 +375,34 @@
         & (iota(shape, 1) % bands // SUBLANES == iota(shape, 0) % LANES // bands)
     ).astype(BF16)
 
-    for load in loads[1:]:
+    for load in loads[:-1]:
         load.wait()
+    pieces, rest = [], occ_ref[:, 0, :]
+    for _ in range(3):
+        pieces.append(rest.astype(BF16).astype(F32))
+        rest = rest - pieces[-1]
+    shape = (3 * modes, wide)
+    occ = dot(
+        jnp.concatenate(pieces, axis=0).astype(BF16),
+        mask(iota(shape, 1) % modes == iota(shape, 0) % modes).astype(BF16), ((0,), (0,)),
+    )
     eye = iota((tiles, tiles), 0) == iota((tiles, tiles), 1)
-    in_block = iota((tiles, n_ka), 0) // slots == iota((tiles, n_ka), 1)
-    live = mask((iota((tiles, 1), 0) % slots).astype(F32) < column(count_ref[...].astype(F32), in_block))
     source_row = source_ref[...].astype(F32)
     target_row = target_ref[...].astype(F32)
-    source = column(source_row, eye)
-    target = column(target_row, eye)
-    shown = window_ref[...].astype(F32) * live
     velocity = velocity_ref[...]
     lifetime = lifetime_ref[...]
     long_lifetime = jnp.concatenate([lifetime] * directions, axis=0)
-
-    copies = mask(iota((span, tiles), 0) // SUBLANES == iota((span, tiles), 1)).astype(BF16)
-    shown = dot(copies, shown.astype(BF16))
-    shown = jnp.where(iota(shown.shape, 1) % SUBLANES == iota(shown.shape, 0) % SUBLANES, shown, 0.0).astype(BF16)
-    shown = dot(shown, mask(iota((bands, LANES), 0) // SUBLANES == iota((bands, LANES), 1) // bands).astype(BF16))
-
+    pick = mask(column(source_row, eye) == iota((tiles, width), 1).astype(F32)).astype(BF16)
     start = (long_lifetime * velocity).astype(BF16)
     start = jnp.concatenate(
         [start[i * bands : (i + 1) * bands] for i in range(directions) for _ in range(outer)], axis=0
     )
-    long_source = column(source_row, iota((span, tiles), 0) // SUBLANES == iota((span, tiles), 1))
-    long_pick = mask(long_source == iota((span, width), 1).astype(F32)).astype(BF16)
-    start = dot(long_pick, start, ((1,), (1,)))
-
-    both = jnp.concatenate([velocity, lifetime], axis=0)
-    pieces = []
-    for _ in range(3):
-        pieces.append(both.astype(BF16))
-        both = both - pieces[-1].astype(F32)
-    pick = mask(source == iota((tiles, width), 1).astype(F32)).astype(BF16)
-    both = dot(pick, jnp.concatenate(pieces, axis=0), ((1,), (1,)))
-    side_send[:tiles] = both[:, 2 * LANES :] + both[:, LANES : 2 * LANES] + both[:, :LANES]
-    shape = (SUBLANES, LANES)
-    side_send[tiles:] = jnp.where(
-        (iota(shape, 0) == 0) & (iota(shape, 1) // tiles == group),
-        jnp.broadcast_to(jnp.concatenate([target_row] * groups, axis=1), shape), 0.0,
-    )
-    key = source + (level * width).astype(F32)
-    bulk_send[SUBLANES * tiles :] = jnp.broadcast_to(key, (tiles, LANES)).astype(BF16)
-
-    shape = (modes, wide)
-    occ = dot(
-        occ_ref[:, 0, :], mask(iota(shape, 1) % modes == iota(shape, 0)), ((0,), (0,)), lax.Precision.HIGHEST
-    )
-    loads[0].wait()
+    start = dot(pick, start, ((1,), (1,)))
+    target = column(target_row, eye)
+    in_block = iota((tiles, n_ka), 0) // slots == iota((tiles, n_ka), 1)
+    live = mask((iota((tiles, 1), 0) % slots).astype(F32) < column(count_ref[...].astype(F32), in_block))
+
+    loads[-1].wait()
     rows = [[] for _ in range(outer)]
     for tile in range(tiles):
         value = coupling_ref[tile].astype(F32)
@@ -406,46 +410,77 @@
         for at in range(outer):
             rows[at].append(value[at * SUBLANES : (at + 1) * SUBLANES])
     rows = jnp.concatenate([jnp.concatenate(part, axis=0).astype(BF16) for part in rows], axis=1)
-    weight = (dot(rows, gather_ref[...]) * shown).astype(BF16).astype(F32)
-    rows_ref[0] = weight
-    rows = jnp.concatenate(
-        [(weight * start[:, i * LANES : (i + 1) * LANES]).astype(BF16) for i in range(directions)], axis=1
-    )
-    rows_ref[1] = dot(rows, reduce)
+    weight = dot(rows, gather_ref[...]).astype(BF16).astype(F32)
+    rows = []
+    for i in range(directions):
+        part = [
+            weight[tile * SUBLANES : (tile + 1) * SUBLANES] * start[tile : tile + 1, i * LANES : (i + 1) * LANES]
+            for tile in range(tiles)
+        ]
+        rows.append(jnp.concatenate(part, axis=0).astype(BF16))
+    rows_ref[1] = dot(jnp.concatenate(rows, axis=1), reduce)
+
+    shown = (window_ref[...].astype(F32) * live).astype(BF16)
+    spread = mask(iota((bands, LANES), 0) == iota((bands, LANES), 1) % bands).astype(BF16)
     lane = iota((tiles, LANES), 1)
-    terms = jnp.where(lane == used, target, 0.0)
+    terms = jnp.zeros((tiles, LANES), F32)
     for at in range(SUBLANES):
-        part = rows_ref[1, pl.ds(at, tiles, stride=SUBLANES), :]
-        terms = jnp.where((lane % SUBLANES == at) & (lane < used), part, terms)
+        terms = jnp.where(lane % SUBLANES == at, rows_ref[1, pl.ds(at, tiles, stride=SUBLANES), :], terms)
+    terms = jnp.where(lane < used, terms * dot(shown, spread), jnp.where(lane == used, target, 0.0))
+    terms = terms.astype(BF16).reshape(HALVES, depth, ny, nc, slots, LANES)
+    for x, yy, hh in owner_list:
+        first_send[(x * ny + yy) * HALVES + hh] = terms[hh, :, yy, x]
+
+    copies = mask(iota((span, tiles), 0) // SUBLANES == iota((span, tiles), 1)).astype(BF16)
+    shown = dot(copies, shown)
+    shown = jnp.where(iota(shown.shape, 1) % SUBLANES == iota(shown.shape, 0) % SUBLANES, shown, 0.0)
+    here = mask(iota((bands, LANES), 0) // SUBLANES == iota((bands, LANES), 1) // bands)
+    rows_ref[0] = weight * dot(shown.astype(BF16), here.astype(BF16))
+    for at in range(SUBLANES):
         bulk_send[at * tiles : (at + 1) * tiles] = rows_ref[0, pl.ds(at, tiles, stride=SUBLANES), :].astype(BF16)
-    first_send[...] = terms.astype(BF16).reshape(first_send.shape)
-
-    @pl.when(is_owner)
-    def _():
-        pl.semaphore_wait(barrier, devices - 1)
-
-    @pl.when(jnp.logical_not(is_owner))
-    def _():
-        pl.semaphore_wait(barrier, owners)
-
-    def local_or_remote(local, src, dst, sent, came, to):
-        @pl.when(local)
-        def _():
-            pltpu.make_async_copy(src, dst, came).start()
-
-        @pl.when(jnp.logical_not(local))
-        def _():
-            remote(src, dst, sent, came, to)
-
-    for dx, dy, dh in owner_steps:
-        x, yy, hh = at_x[dx], at_y[dy], at_half[dh]
-        args = (first_send.at[hh, :, yy, x], recv.at[0, host, p, level], send_sem.at[0], recv_sem.at[0], owner_at(x, yy, hh))
-        if dx or dy or dh:
-            remote(*args)
-        else:
-            local_or_remote(is_owner, *args)
+
+    both = jnp.concatenate([velocity, lifetime], axis=0)
+    pieces = []
+    for _ in range(3):
+        pieces.append(both.astype(BF16))
+        both = both - pieces[-1].astype(F32)
+    both = dot(pick, jnp.concatenate(pieces, axis=0), ((1,), (1,)))
+    side_send[:tiles] = both[:, 2 * LANES :] + both[:, LANES : 2 * LANES] + both[:, :LANES]
+    shape = (SUBLANES, LANES)
+    long_target = jnp.broadcast_to(jnp.concatenate([target_row] * groups, axis=1), shape)
+    long_source = jnp.broadcast_to(jnp.concatenate([source_row] * groups, axis=1), shape)
+    long_source = long_source + (level * width).astype(F32)
+    tail = jnp.where(iota(shape, 0) == 0, long_target, jnp.where(iota(shape, 0) == 1, long_source, 0.0))
+    side_send[tiles:] = jnp.where(iota(shape, 1) // tiles == group, tail, 0.0)
     keeper = owner_at(c, y, half)
     stays = is_owner & (c == p)
+
+    @pl.when(is_owner)
+    def _():
+        pl.semaphore_wait(barrier, owners - 1)
+
+    @pl.when(is_other)
+    def _():
+        pl.semaphore_wait(barrier, owners)
+
+    @pl.when(is_other)
+    def _():
+        for x, yy, hh in owner_list:
+            remote(
+                first_send.at[(x * ny + yy) * HALVES + hh], recv.at[0, host, group], send_sem.at[0], recv_sem.at[0],
+                owner_at(x, yy, hh),
+            )
+
+    @pl.when(is_owner)
+    def _():
+        for dx, dy, dh in owner_steps:
+            x, yy, hh = at_x[dx], at_y[dy], at_half[dh]
+            src, dst = first_send.at[(x * ny + yy) * HALVES + hh], recv.at[0, host, group]
+            if dx or dy or dh:
+                remote(src, dst, send_sem.at[0], recv_sem.at[0], owner_at(x, yy, hh))
+            else:
+                pltpu.make_async_copy(src, dst, recv_sem.at[0]).start()
+
     local_or_remote(stays, side_send, side_recv.at[group], side_sems.at[0], side_sems.at[1], keeper)
     local_or_remote(stays, bulk_send, bulk_recv.at[group], bulk_sems.at[0], bulk_sems.at[1], keeper)
 
@@ -455,23 +490,23 @@
         both = side_recv[:, :tiles].reshape(LANES, LANES).T
         velocity = both[:used]
         lifetime = jnp.concatenate([both[used:]] * directions, axis=0)
-        target_rows = side_recv[0, tiles:]
+        tail = side_recv[0, tiles:]
         for at in range(1, groups):
-            target_rows = target_rows + side_recv[at, tiles:]
-        tail = jnp.concatenate([target_rows, jnp.zeros((LANES - used - SUBLANES, LANES), F32)], axis=0)
+            tail = tail + side_recv[at, tiles:]
+        below = jnp.where(iota(tail.shape, 0) == 0, tail, 0.0)
+        below = jnp.concatenate([below, jnp.zeros((LANES - used - SUBLANES, LANES), F32)], axis=0)
         choose = None
         for step in range(1, ITERS):
             await_bytes(recv.at[step - 1], recv_sem.at[step - 1])
             arrived = recv[step - 1].reshape(LANES, LANES).T
             if step == 1:
-                row_key = arrived[used : used + 1].astype(F32)
-                row_key = row_key + (iota((1, LANES), 1) // slots % depth * width).astype(F32)
-                await_bytes(bulk_recv, bulk_sems.at[1])
-                key = bulk_recv[:, SUBLANES * tiles :].reshape(LANES, LANES).astype(F32)
-                choose = mask(key == row_key).astype(BF16)
-            value = lifetime * (velocity + dot(arrived[:used], choose, ((1,), (1,))))
+                row_key = recv[0].reshape(LANES, LANES)[:, used : used + 1].astype(F32)
+                row_key = row_key + (iota((LANES, 1), 0) // slots % depth * width).astype(F32)
+                choose = mask(row_key == tail[1:2]).astype(BF16)
+            value = lifetime * (velocity + dot(arrived[:used], choose))
             value = value.astype(BF16).astype(F32)
             if step == 1:
+                await_bytes(bulk_recv, bulk_sems.at[1])
                 for at in range(SUBLANES):
                     part = bulk_recv[:, at * tiles : (at + 1) * tiles].reshape(LANES, LANES).T
                     weight_ref[at * LANES : (at + 1) * LANES] = part.astype(F32)
@@ -490,25 +525,31 @@
                         parts[i].append(totals[i])
                 for i in range(directions):
                     terms[i].append(fold_rows(parts[i]))
-            terms = jnp.concatenate([part for found in terms for part in found] + [tail], axis=0)
-            terms_send[step - 1] = terms.astype(BF16).T.reshape(terms_send.shape[1:])
+            terms = jnp.concatenate([part for found in terms for part in found] + [below], axis=0)
+            terms = terms.astype(BF16).T.reshape(groups, HALVES, depth, ny, nc, slots, LANES)
             if step < ITERS - 1:
+                for x, yy, hh in owner_list:
+                    terms_send[step - 1, (x * ny + yy) * HALVES + hh] = terms[:, hh, :, yy, x]
                 for dx, dy, dh in owner_steps:
                     x, yy, hh = at_x[dx], at_y[dy], at_half[dh]
-                    src, dst = terms_send.at[step - 1, :, hh, :, yy, x], recv.at[step, mine].reshape(groups, depth, slots, LANES)
+                    src, dst = terms_send.at[step - 1, (x * ny + yy) * HALVES + hh], recv.at[step, mine]
                     if dx or dy or dh:
                         remote(src, dst, send_sem.at[step], recv_sem.at[step], owner_at(x, yy, hh))
                     else:
                         pltpu.make_async_copy(src, dst, recv_sem.at[step]).start()
             else:
-                for dx, dy, dz, dc in all_steps:
-                    x, yy, zz, cc = at_x[dx], at_y[dy], at_z[dz], at_c[dc]
-                    src = terms_send.at[step - 1, :, lax.div(zz, depth), lax.rem(zz, depth), yy, cc]
-                    dst = last_recv.at[mine]
-                    if dx or dy or dz or dc:
-                        remote(src, dst, send_sem.at[step], recv_sem.at[step], device_at(x, yy, zz, cc))
+                for at in range(n_ka):
+                    zz, yy, cc = at // (ny * nc), at // nc % ny, at % nc
+                    last_send[at] = terms[:, zz // depth, zz % depth, yy, cc]
+
+                def act(spot, is_here):
+                    src, dst = last_send.at[(spot[2] * ny + spot[1]) * nc + spot[3]], last_recv.at[mine]
+                    if is_here:
+                        pltpu.make_async_copy(src, dst, recv_sem.at[step]).start()
                     else:
-                        pltpu.make_async_copy(src, dst, recv_sem.at[step]).start()
+                        remote(src, dst, send_sem.at[step], recv_sem.at[step], device_at(*spot))
+
+                per_device(act)
 
     await_bytes(last_recv, recv_sem.at[ITERS - 1])
     arrived = last_recv[...].reshape(devices * slots, LANES).T
@@ -519,16 +560,16 @@
 
     @pl.when(is_owner)
     def _():
-        await_bytes(recv.at[0, pl.ds(0, owners - 1), 0, 0], send_sem.at[0])
+        await_bytes(recv.at[0, pl.ds(0, owners - 1), 0], send_sem.at[0])
         for step in range(1, ITERS - 1):
             await_bytes(recv.at[step, pl.ds(0, owners - 1)], send_sem.at[step])
         for _ in range(groups - 1):
             await_bytes(last_recv, send_sem.at[ITERS - 1])
         await_bytes(last_recv.at[pl.ds(0, owners - 1)], send_sem.at[ITERS - 1])
 
-    @pl.when(jnp.logical_not(is_owner))
-    def _():
-        await_bytes(recv.at[0, :, 0, 0], send_sem.at[0])
+    @pl.when(is_other)
+    def _():
+        await_bytes(recv.at[0, :, 0], send_sem.at[0])
 
     @pl.when(jnp.logical_not(stays))
     def _():
@@ -586,13 +627,14 @@
             pltpu.VMEM((bands // SUBLANES * coupling.shape[-1], LANES), BF16),
             pltpu.VMEM((2, tiles * SUBLANES, LANES), F32),
             pltpu.VMEM((SUBLANES * LANES, LANES), F32),
-            pltpu.VMEM((HALVES, depth, ny, nc, slots, LANES), BF16),
-            pltpu.VMEM(((SUBLANES + 1) * tiles, LANES), BF16),
+            pltpu.VMEM((owners, depth, slots, LANES), BF16),
+            pltpu.VMEM((SUBLANES * tiles, LANES), BF16),
             pltpu.VMEM((tiles + SUBLANES, LANES), F32),
-            pltpu.VMEM((groups, (SUBLANES + 1) * tiles, LANES), BF16),
+            pltpu.VMEM((groups, SUBLANES * tiles, LANES), BF16),
             pltpu.VMEM((groups, tiles + SUBLANES, LANES), F32),
-            pltpu.VMEM((ITERS - 1, groups, HALVES, depth, ny, nc, slots, LANES), BF16),
-            pltpu.VMEM((ITERS - 1, owners, nx, depth, depth, slots, LANES), BF16),
+            pltpu.VMEM((ITERS - 2, owners, groups, depth, slots, LANES), BF16),
+            pltpu.VMEM((ITERS - 1, owners, groups, depth, slots, LANES), BF16),
+            pltpu.VMEM((nz * ny * nc, groups, slots, LANES), BF16),
             pltpu.VMEM((owners, groups, slots, LANES), BF16),
             pltpu.SemaphoreType.DMA((len(operands),)),
             pltpu.SemaphoreType.DMA((2,)),

time: 20.9 us -> 20.5 us (0.981)
  Pallas kernels: 20.2 us -> 19.7 us
    pallas_call x1, Pallas kernels: 20.2 us -> 19.7 us  [owner_shards(): pl.pallas_call(functools.partial(owner_kernel, grid, directions), out_sha...]
where the time goes in v2:
time: 20.5 us; the launch traced here: 20.3 us
  Pallas kernels  19.7 us (96%)
  local copies, waits for them, and re-layouts  0.62 us (3%)
    pallas_call x1, Pallas kernels, owner_shards(): pl.pallas_call(functools.partial(owner_kernel, grid, directions), out_sha...  19.7 us
    unnamed x1, local copies, waits for them, and re-layouts  0.62 us

profile of v2, /device:TPU:0, one launch (start us, length us, event | category | flops | bytes accessed | tf_op | source)
XLA Modules:
  0.0 20.3 jit_solution(8945038034482047883)
XLA Ops:
  0.0 19.7 %shard_map.82 = f32[96,128]{1,0:T(8,128)S(1)} custom-call(bf16[32,32,384]{2,1,0:T(8,128)(2,1)} %bitcast.11, f32[12,1,32]{2,1,0:T(1,128)} %bitcast.14, s32[32,32]{1,0:T(8,128)} %bitcast.13, s32[1,16]{1,0:T(1,128)} %bitcast.15, s32[1,32]{1,0:T(1,128)} %bitcast.16, s32[1,32]{1,0:T(1,128)} %bitcast.17, f32[96,128]{1,0:T(8,128)} %bitcast.12, f32[32,128]{1,0:T(8,128)} %refs_7_.1), custom_call_target="tpu_custom_call" | custom-call | tf_op jit(solution)/shard_map/pallas_call | solution.py:620
  19.7 0.6 %copy.10 = f32[3,32,128]{2,1,0:T(8,128)} copy(f32[3,32,128]{2,1,0:T(8,128)S(1)} %bitcast.10) | data formatting | bytes 98304

commit v3 on v2

--- a/solution.py
+++ b/solution.py
@@ -279,8 +279,9 @@
     *refs,
 ):
     inputs, out_ref, held = refs[:8], refs[8], refs[9:17]
-    (gather_ref, rows_ref, weight_ref, first_send, bulk_send, side_send, bulk_recv, side_recv, terms_send, recv, last_send, last_recv,
-     load_sem, bulk_sems, side_sems, send_sem, recv_sem) = refs[17:]
+    (gather_ref, rows_ref, weight_ref, first_send, bulk_send, side_send, bulk_recv, side_recv, terms_send, recv, last_send, last_recv, first_recv,
+     front_weight_send, front_side_send, part_send, front_weight, front_side, part_recv, long_rows,
+     load_sem, bulk_sems, side_sems, send_sem, recv_sem, front_sems) = refs[17:]
     coupling_ref, occ_ref, window_ref, count_ref, target_ref, source_ref, velocity_ref, lifetime_ref = held
     loads = [pltpu.make_async_copy(x, y, load_sem.at[i]) for i, (x, y) in enumerate(zip(inputs[1:], held[1:]))]
     loads.append(pltpu.make_async_copy(inputs[0], coupling_ref, load_sem.at[len(loads)]))
@@ -308,6 +309,8 @@
     level = lax.rem(z, depth)
     is_owner = (c == nc - 1) & (z == half + (depth - 1))
     is_other = jnp.logical_not(is_owner)
+    is_front = (p == 0) & (y == 0) & (z == 0)
+    is_back = jnp.logical_not(is_front)
     mine = (p * ny + y) * HALVES + half
     host = (c * ny + y) * HALVES + half
     group = p * depth + level
@@ -346,6 +349,14 @@
                 greet(device_at(*spot))
 
         per_device(act)
+
+    @pl.when(is_front)
+    def _():
+        for spot in every:
+            if sum(spot[:3]):
+                greet(device_at(*spot))
+        for at in range(1, nc):
+            greet(device_at(p, y, z, lax.rem(c + at, nc)))
 
     def remote(src, dst, sent, came, to):
         pltpu.make_async_remote_copy(
@@ -392,7 +403,8 @@
     velocity = velocity_ref[...]
     lifetime = lifetime_ref[...]
     long_lifetime = jnp.concatenate([lifetime] * directions, axis=0)
-    pick = mask(column(source_row, eye) == iota((tiles, width), 1).astype(F32)).astype(BF16)
+    source = column(source_row, eye)
+    pick = mask(source == iota((tiles, width), 1).astype(F32)).astype(BF16)
     start = (long_lifetime * velocity).astype(BF16)
     start = jnp.concatenate(
         [start[i * bands : (i + 1) * bands] for i in range(directions) for _ in range(outer)], axis=0
@@ -428,8 +440,10 @@
         terms = jnp.where(lane % SUBLANES == at, rows_ref[1, pl.ds(at, tiles, stride=SUBLANES), :], terms)
     terms = jnp.where(lane < used, terms * dot(shown, spread), jnp.where(lane == used, target, 0.0))
     terms = terms.astype(BF16).reshape(HALVES, depth, ny, nc, slots, LANES)
+    fronts = jnp.broadcast_to(source[: nc * slots], (nc * slots, LANES)).astype(BF16).reshape(nc, slots, LANES)
     for x, yy, hh in owner_list:
-        first_send[(x * ny + yy) * HALVES + hh] = terms[hh, :, yy, x]
+        first_send[(x * ny + yy) * HALVES + hh, :depth] = terms[hh, :, yy, x]
+        first_send[(x * ny + yy) * HALVES + hh, depth:] = fronts
 
     copies = mask(iota((span, tiles), 0) // SUBLANES == iota((span, tiles), 1)).astype(BF16)
     shown = dot(copies, shown)
@@ -439,13 +453,19 @@
     for at in range(SUBLANES):
         bulk_send[at * tiles : (at + 1) * tiles] = rows_ref[0, pl.ds(at, tiles, stride=SUBLANES), :].astype(BF16)
 
+    front_weight_send[...] = rows_ref[0, : nc * slots * SUBLANES].astype(BF16).reshape(front_weight_send.shape)
     both = jnp.concatenate([velocity, lifetime], axis=0)
     pieces = []
     for _ in range(3):
         pieces.append(both.astype(BF16))
         both = both - pieces[-1].astype(F32)
     both = dot(pick, jnp.concatenate(pieces, axis=0), ((1,), (1,)))
-    side_send[:tiles] = both[:, 2 * LANES :] + both[:, LANES : 2 * LANES] + both[:, :LANES]
+    both = both[:, 2 * LANES :] + both[:, LANES : 2 * LANES] + both[:, :LANES]
+    side_send[:tiles] = both
+    for at in range(nc):
+        of = slice(at * slots, (at + 1) * slots)
+        front_side_send[at, :slots] = both[of]
+        front_side_send[at, slots:] = jnp.broadcast_to(target[of], (slots, LANES))
     shape = (SUBLANES, LANES)
     long_target = jnp.broadcast_to(jnp.concatenate([target_row] * groups, axis=1), shape)
     long_source = jnp.broadcast_to(jnp.concatenate([source_row] * groups, axis=1), shape)
@@ -457,17 +477,21 @@
 
     @pl.when(is_owner)
     def _():
-        pl.semaphore_wait(barrier, owners - 1)
-
-    @pl.when(is_other)
-    def _():
-        pl.semaphore_wait(barrier, owners)
+        pl.semaphore_wait(barrier, owners - 1 + nc)
+
+    @pl.when(is_front)
+    def _():
+        pl.semaphore_wait(barrier, owners + nc - 1)
+
+    @pl.when(is_other & is_back)
+    def _():
+        pl.semaphore_wait(barrier, owners + nc)
 
     @pl.when(is_other)
     def _():
         for x, yy, hh in owner_list:
             remote(
-                first_send.at[(x * ny + yy) * HALVES + hh], recv.at[0, host, group], send_sem.at[0], recv_sem.at[0],
+                first_send.at[(x * ny + yy) * HALVES + hh], first_recv.at[host, group], send_sem.at[0], recv_sem.at[0],
                 owner_at(x, yy, hh),
             )
 
@@ -475,7 +499,7 @@
     def _():
         for dx, dy, dh in owner_steps:
             x, yy, hh = at_x[dx], at_y[dy], at_half[dh]
-            src, dst = first_send.at[(x * ny + yy) * HALVES + hh], recv.at[0, host, group]
+            src, dst = first_send.at[(x * ny + yy) * HALVES + hh], first_recv.at[host, group]
             if dx or dy or dh:
                 remote(src, dst, send_sem.at[0], recv_sem.at[0], owner_at(x, yy, hh))
             else:
@@ -483,7 +507,35 @@
 
     local_or_remote(stays, side_send, side_recv.at[group], side_sems.at[0], side_sems.at[1], keeper)
     local_or_remote(stays, bulk_send, bulk_recv.at[group], bulk_sems.at[0], bulk_sems.at[1], keeper)
-
+    from_here = host * groups + group
+    for at in range(nc):
+        to, here = device_at(0, 0, 0, at), is_front & (c == at)
+        local_or_remote(
+            here, front_weight_send.at[at], front_weight.at[from_here], front_sems.at[0], front_sems.at[1], to
+        )
+        local_or_remote(
+            here, front_side_send.at[at], front_side.at[from_here], front_sems.at[2], front_sems.at[3], to
+        )
+
+    def multiply(value):
+        terms = [[] for _ in range(directions)]
+        for at in range(outer):
+            parts = [[] for _ in range(directions)]
+            for inner in range(SUBLANES):
+                totals = [None] * directions
+                for m in range(0, bands, SUBLANES):
+                    first = inner * LANES + at * bands + m
+                    factor = weight_ref[first : first + SUBLANES]
+                    for i in range(directions):
+                        term = factor * value[i * bands + m : i * bands + m + SUBLANES]
+                        totals[i] = term if totals[i] is None else totals[i] + term
+                for i in range(directions):
+                    parts[i].append(totals[i])
+            for i in range(directions):
+                terms[i].append(fold_rows(parts[i]))
+        return jnp.concatenate([part for found in terms for part in found], axis=0)
+
+    singles = devices * slots
     @pl.when(is_owner)
     def _():
         await_bytes(side_recv, side_sems.at[1])
@@ -497,12 +549,16 @@
         below = jnp.concatenate([below, jnp.zeros((LANES - used - SUBLANES, LANES), F32)], axis=0)
         choose = None
         for step in range(1, ITERS):
-            await_bytes(recv.at[step - 1], recv_sem.at[step - 1])
-            arrived = recv[step - 1].reshape(LANES, LANES).T
             if step == 1:
-                row_key = recv[0].reshape(LANES, LANES)[:, used : used + 1].astype(F32)
+                await_bytes(first_recv, recv_sem.at[0])
+                arrived = first_recv[:, :, :depth].reshape(LANES, LANES)
+                row_key = arrived[:, used : used + 1].astype(F32)
                 row_key = row_key + (iota((LANES, 1), 0) // slots % depth * width).astype(F32)
                 choose = mask(row_key == tail[1:2]).astype(BF16)
+                arrived = arrived.T
+            else:
+                await_bytes(recv.at[step - 2], recv_sem.at[step - 1])
+                arrived = recv[step - 2].reshape(LANES, LANES).T
             value = lifetime * (velocity + dot(arrived[:used], choose))
             value = value.astype(BF16).astype(F32)
             if step == 1:
@@ -510,39 +566,44 @@
                 for at in range(SUBLANES):
                     part = bulk_recv[:, at * tiles : (at + 1) * tiles].reshape(LANES, LANES).T
                     weight_ref[at * LANES : (at + 1) * LANES] = part.astype(F32)
-            terms = [[] for _ in range(directions)]
-            for at in range(outer):
-                parts = [[] for _ in range(directions)]
-                for inner in range(SUBLANES):
-                    totals = [None] * directions
-                    for m in range(0, bands, SUBLANES):
-                        first = inner * LANES + at * bands + m
-                        factor = weight_ref[first : first + SUBLANES]
-                        for i in range(directions):
-                            term = factor * value[i * bands + m : i * bands + m + SUBLANES]
-                            totals[i] = term if totals[i] is None else totals[i] + term
-                    for i in range(directions):
-                        parts[i].append(totals[i])
-                for i in range(directions):
-                    terms[i].append(fold_rows(parts[i]))
-            terms = jnp.concatenate([part for found in terms for part in found] + [below], axis=0)
-            terms = terms.astype(BF16).T.reshape(groups, HALVES, depth, ny, nc, slots, LANES)
+            terms = jnp.concatenate([multiply(value), below], axis=0).astype(BF16).T
+            flat, terms = terms, terms.reshape(groups, HALVES, depth, ny, nc, slots, LANES)
             if step < ITERS - 1:
                 for x, yy, hh in owner_list:
                     terms_send[step - 1, (x * ny + yy) * HALVES + hh] = terms[:, hh, :, yy, x]
                 for dx, dy, dh in owner_steps:
                     x, yy, hh = at_x[dx], at_y[dy], at_half[dh]
-                    src, dst = terms_send.at[step - 1, (x * ny + yy) * HALVES + hh], recv.at[step, mine]
+                    src, dst = terms_send.at[step - 1, (x * ny + yy) * HALVES + hh], recv.at[step - 1, mine]
                     if dx or dy or dh:
                         remote(src, dst, send_sem.at[step], recv_sem.at[step], owner_at(x, yy, hh))
                     else:
                         pltpu.make_async_copy(src, dst, recv_sem.at[step]).start()
+                if step == 1:
+                    lane_tile = iota((1, LANES), 1) % tiles
+                    row_key = tail[:1] + (lane_tile // slots * width).astype(F32)
+                    at = iota((singles, 1), 0) // slots
+                    of, at = at % groups % depth, at // groups
+                    block = ((at % HALVES * depth + of) * ny + at // HALVES % ny) * nc + at // (HALVES * ny)
+                    block = (block * width).astype(F32)
+                    wanted = [
+                        first_recv[:, :, depth + i].reshape(singles, LANES).astype(F32) + block for i in range(nc)
+                    ]
+                    wanted = mask(jnp.concatenate(wanted, axis=0) == row_key).astype(BF16)
+                if step == ITERS - 2:
+                    part_send[...] = dot(wanted, flat).astype(BF16).reshape(part_send.shape)
+                    for i in range(nc):
+                        remote(
+                            part_send.at[i], part_recv.at[mine], front_sems.at[4], front_sems.at[5],
+                            device_at(0, 0, 0, i),
+                        )
             else:
                 for at in range(n_ka):
                     zz, yy, cc = at // (ny * nc), at // nc % ny, at % nc
                     last_send[at] = terms[:, zz // depth, zz % depth, yy, cc]
 
                 def act(spot, is_here):
+                    if not sum(spot[:3]):
+                        return
                     src, dst = last_send.at[(spot[2] * ny + spot[1]) * nc + spot[3]], last_recv.at[mine]
                     if is_here:
                         pltpu.make_async_copy(src, dst, recv_sem.at[step]).start()
@@ -551,25 +612,60 @@
 
                 per_device(act)
 
-    await_bytes(last_recv, recv_sem.at[ITERS - 1])
-    arrived = last_recv[...].reshape(devices * slots, LANES).T
-    scatter = mask(
-        arrived[used : used + 1].astype(F32) == iota((width, devices * slots), 0).astype(F32)
-    ).astype(BF16)
-    out_ref[...] = long_lifetime * (velocity + dot(arrived[:used], scatter, ((1,), (1,))))
+    @pl.when(is_front)
+    def _():
+        await_bytes(front_weight, front_sems.at[1])
+        await_bytes(front_side, front_sems.at[3])
+        long_rows[...] = front_weight[...].reshape(long_rows.shape).astype(F32)
+        blank = jnp.zeros((LANES - singles, LANES), F32)
+        for at in range(SUBLANES):
+            part = jnp.concatenate([long_rows[pl.ds(at, singles, stride=SUBLANES), :], blank], axis=0)
+            weight_ref[at * LANES : (at + 1) * LANES] = part.T
+        both = front_side[:, :slots].reshape(singles, LANES)
+        scale = jnp.concatenate([both, blank], axis=0).T[used:]
+        scale = jnp.concatenate([scale] * directions + [jnp.zeros_like(scale)], axis=0).T[:singles]
+        place = front_side[:, slots:].reshape(singles, LANES) == iota((singles, width), 1).astype(F32)
+        place = jnp.concatenate([mask(place), blank], axis=0).astype(BF16)
+        await_bytes(part_recv, front_sems.at[5])
+        total = part_recv[0].astype(F32)
+        for at in range(1, owners):
+            total = total + part_recv[at].astype(F32)
+        value = jnp.concatenate([scale * (both + total), blank], axis=0).astype(BF16).T.astype(F32)
+        terms = dot(multiply(value[:used]).astype(BF16), place)
+        out_ref[...] = long_lifetime * (velocity + terms)
+
+    @pl.when(is_back)
+    def _():
+        await_bytes(last_recv, recv_sem.at[ITERS - 1])
+        arrived = last_recv[...].reshape(singles, LANES).T
+        scatter = mask(arrived[used : used + 1].astype(F32) == iota((width, singles), 0).astype(F32)).astype(BF16)
+        out_ref[...] = long_lifetime * (velocity + dot(arrived[:used], scatter, ((1,), (1,))))
 
     @pl.when(is_owner)
     def _():
-        await_bytes(recv.at[0, pl.ds(0, owners - 1), 0], send_sem.at[0])
+        await_bytes(first_send.at[pl.ds(0, owners - 1)], send_sem.at[0])
         for step in range(1, ITERS - 1):
-            await_bytes(recv.at[step, pl.ds(0, owners - 1)], send_sem.at[step])
-        for _ in range(groups - 1):
+            await_bytes(terms_send.at[step - 1, pl.ds(0, owners - 1)], send_sem.at[step])
+        sent = devices - nc - 1
+        for _ in range(sent // owners):
             await_bytes(last_recv, send_sem.at[ITERS - 1])
-        await_bytes(last_recv.at[pl.ds(0, owners - 1)], send_sem.at[ITERS - 1])
+        if sent % owners:
+            await_bytes(last_recv.at[pl.ds(0, sent % owners)], send_sem.at[ITERS - 1])
+        await_bytes(part_send, front_sems.at[4])
 
     @pl.when(is_other)
     def _():
-        await_bytes(recv.at[0, :, 0], send_sem.at[0])
+        await_bytes(first_send, send_sem.at[0])
+
+    for ref, semaphore in ((front_weight_send, front_sems.at[0]), (front_side_send, front_sems.at[2])):
+
+        @pl.when(is_front)
+        def _():
+            await_bytes(ref.at[pl.ds(0, nc - 1)], semaphore)
+
+        @pl.when(is_back)
+        def _():
+            await_bytes(ref, semaphore)
 
     @pl.when(jnp.logical_not(stays))
     def _():
@@ -589,7 +685,7 @@
         for a, spot in enumerate(row):
             if tuple(s - l for s, l in zip(spot, low)) != (p, a // nc % ny, a // (nc * ny), a % nc):
                 return None
-    return sizes if nx == nc and nz % HALVES == 0 else None
+    return sizes if nx == nc and nc > 1 and nz % HALVES == 0 and nz > HALVES else None
 
 
 def fits(grid, coupling, velocity):
@@ -600,7 +696,7 @@
     directions, bands, width = velocity.shape
     depth = nz // HALVES
     return (
-        nx * depth * tiles == LANES and bands * bands == SUBLANES * LANES and (directions + 1) * bands == LANES
+        nx * depth * tiles == LANES and nc * nx * tiles <= LANES and bands * bands == SUBLANES * LANES and (directions + 1) * bands == LANES
         and depth * width <= 256 and width == LANES
     )
 
@@ -613,6 +709,7 @@
     depth = nz // HALVES
     groups = nx * depth
     owners = nc * ny * HALVES
+    singles = nx * nz * ny * nc * slots
     operands = (
         coupling[0, 0], jnp.transpose(phonon_occ[0], (2, 0, 1)), band_window[0, 0], pair_count[0], k_target[0],
         kq_source[0], velocity.reshape(directions * bands, width), lifetime,
@@ -627,20 +724,29 @@
             pltpu.VMEM((bands // SUBLANES * coupling.shape[-1], LANES), BF16),
             pltpu.VMEM((2, tiles * SUBLANES, LANES), F32),
             pltpu.VMEM((SUBLANES * LANES, LANES), F32),
-            pltpu.VMEM((owners, depth, slots, LANES), BF16),
+            pltpu.VMEM((owners, depth + nc, slots, LANES), BF16),
             pltpu.VMEM((SUBLANES * tiles, LANES), BF16),
             pltpu.VMEM((tiles + SUBLANES, LANES), F32),
             pltpu.VMEM((groups, SUBLANES * tiles, LANES), BF16),
             pltpu.VMEM((groups, tiles + SUBLANES, LANES), F32),
             pltpu.VMEM((ITERS - 2, owners, groups, depth, slots, LANES), BF16),
-            pltpu.VMEM((ITERS - 1, owners, groups, depth, slots, LANES), BF16),
+            pltpu.VMEM((ITERS - 2, owners, groups, depth, slots, LANES), BF16),
             pltpu.VMEM((nz * ny * nc, groups, slots, LANES), BF16),
             pltpu.VMEM((owners, groups, slots, LANES), BF16),
+            pltpu.VMEM((owners, groups, depth + nc, slots, LANES), BF16),
+            pltpu.VMEM((nc, slots * SUBLANES, LANES), BF16),
+            pltpu.VMEM((nc, 2 * slots, LANES), F32),
+            pltpu.VMEM((nc, singles, LANES), BF16),
+            pltpu.VMEM((owners * groups, slots * SUBLANES, LANES), BF16),
+            pltpu.VMEM((owners * groups, 2 * slots, LANES), F32),
+            pltpu.VMEM((owners, singles, LANES), BF16),
+            pltpu.VMEM((singles * SUBLANES, LANES), F32),
             pltpu.SemaphoreType.DMA((len(operands),)),
             pltpu.SemaphoreType.DMA((2,)),
             pltpu.SemaphoreType.DMA((2,)),
             pltpu.SemaphoreType.DMA((ITERS,)),
             pltpu.SemaphoreType.DMA((ITERS,)),
+            pltpu.SemaphoreType.DMA((6,)),
         ],
         compiler_params=pltpu.CompilerParams(collective_id=0, has_side_effects=True),
     )(*operands)

time: 20.5 us -> 19.6 us (0.956)
  the two profiles are of different devices: /device:TPU:0 before, /device:TPU:3 now
where the time goes in v3:
time: 19.6 us; the launch traced here: 19.4 us
  Pallas kernels  18.8 us (96%)
  local copies, waits for them, and re-layouts  0.62 us (3%)
    pallas_call x1, Pallas kernels, owner_shards(): pl.pallas_call(functools.partial(owner_kernel, grid, directions), out_sha...  18.8 us
    unnamed x1, local copies, waits for them, and re-layouts  0.62 us

profile of v3, /device:TPU:3, one launch (start us, length us, event | category | flops | bytes accessed | tf_op | source)
XLA Modules:
  0.0 19.4 jit_solution(12733936641499397657)
XLA Ops:
  0.0 18.8 %shard_map.82 = f32[96,128]{1,0:T(8,128)S(1)} custom-call(bf16[32,32,384]{2,1,0:T(8,128)(2,1)} %bitcast.11, f32[12,1,32]{2,1,0:T(1,128)} %bitcast.14, s32[32,32]{1,0:T(8,128)} %bitcast.13, s32[1,16]{1,0:T(1,128)} %bitcast.15, s32[1,32]{1,0:T(1,128)} %bitcast.16, s32[1,32]{1,0:T(1,128)} %bitcast.17, f32[96,128]{1,0:T(8,128)} %bitcast.12, f32[32,128]{1,0:T(8,128)} %refs_7_.1), custom_call_target="tpu_custom_call" | custom-call | tf_op jit(solution)/shard_map/pallas_call | solution.py:717
  18.8 0.6 %copy.10 = f32[3,32,128]{2,1,0:T(8,128)} copy(f32[3,32,128]{2,1,0:T(8,128)S(1)} %bitcast.10) | data formatting | bytes 98304

commit v4 on v3

--- a/solution.py
+++ b/solution.py
@@ -309,7 +309,7 @@
     level = lax.rem(z, depth)
     is_owner = (c == nc - 1) & (z == half + (depth - 1))
     is_other = jnp.logical_not(is_owner)
-    is_front = (p == 0) & (y == 0) & (z == 0)
+    is_front = (y == 0) & (z == 0)
     is_back = jnp.logical_not(is_front)
     mine = (p * ny + y) * HALVES + half
     host = (c * ny + y) * HALVES + half
@@ -320,6 +320,8 @@
     owner_list = [spot for pair in zip(owner_list, owner_list[::-1]) for spot in pair][: len(owner_list)]
     every = [(x, yy, zz, cc) for zz in range(nz) for yy in range(ny) for x in range(nx) for cc in range(nc)]
     every = sorted(every, key=lambda spot: sum(spot[:3]))
+    front_list = [spot for spot in every if not spot[1] and not spot[2]]
+    blocks = nc
 
     def owner_at(x, y, half):
         return {"pb": x, "ka": ((half + (depth - 1)) * ny + y) * nc + (nc - 1)}
@@ -352,11 +354,11 @@
 
     @pl.when(is_front)
     def _():
-        for spot in every:
-            if sum(spot[:3]):
-                greet(device_at(*spot))
-        for at in range(1, nc):
-            greet(device_at(p, y, z, lax.rem(c + at, nc)))
+        for x, yy, zz, cc in every:
+            if yy or zz:
+                greet(device_at(x, yy, zz, cc))
+            else:
+                pl.when((p != x) | (c != cc))(functools.partial(greet, device_at(x, yy, zz, cc)))
 
     def remote(src, dst, sent, came, to):
         pltpu.make_async_remote_copy(
@@ -440,7 +442,8 @@
         terms = jnp.where(lane % SUBLANES == at, rows_ref[1, pl.ds(at, tiles, stride=SUBLANES), :], terms)
     terms = jnp.where(lane < used, terms * dot(shown, spread), jnp.where(lane == used, target, 0.0))
     terms = terms.astype(BF16).reshape(HALVES, depth, ny, nc, slots, LANES)
-    fronts = jnp.broadcast_to(source[: nc * slots], (nc * slots, LANES)).astype(BF16).reshape(nc, slots, LANES)
+    fronts = jnp.broadcast_to(source[: blocks * slots], (blocks * slots, LANES)).astype(BF16)
+    fronts = fronts.reshape(blocks, slots, LANES)
     for x, yy, hh in owner_list:
         first_send[(x * ny + yy) * HALVES + hh, :depth] = terms[hh, :, yy, x]
         first_send[(x * ny + yy) * HALVES + hh, depth:] = fronts
@@ -453,7 +456,7 @@
     for at in range(SUBLANES):
         bulk_send[at * tiles : (at + 1) * tiles] = rows_ref[0, pl.ds(at, tiles, stride=SUBLANES), :].astype(BF16)
 
-    front_weight_send[...] = rows_ref[0, : nc * slots * SUBLANES].astype(BF16).reshape(front_weight_send.shape)
+    front_weight_send[...] = rows_ref[0, : blocks * slots * SUBLANES].astype(BF16).reshape(front_weight_send.shape)
     both = jnp.concatenate([velocity, lifetime], axis=0)
     pieces = []
     for _ in range(3):
@@ -462,7 +465,7 @@
     both = dot(pick, jnp.concatenate(pieces, axis=0), ((1,), (1,)))
     both = both[:, 2 * LANES :] + both[:, LANES : 2 * LANES] + both[:, :LANES]
     side_send[:tiles] = both
-    for at in range(nc):
+    for at in range(blocks):
         of = slice(at * slots, (at + 1) * slots)
         front_side_send[at, :slots] = both[of]
         front_side_send[at, slots:] = jnp.broadcast_to(target[of], (slots, LANES))
@@ -477,15 +480,15 @@
 
     @pl.when(is_owner)
     def _():
-        pl.semaphore_wait(barrier, owners - 1 + nc)
+        pl.semaphore_wait(barrier, owners - 1 + len(front_list))
 
     @pl.when(is_front)
     def _():
-        pl.semaphore_wait(barrier, owners + nc - 1)
+        pl.semaphore_wait(barrier, owners + len(front_list) - 1)
 
     @pl.when(is_other & is_back)
     def _():
-        pl.semaphore_wait(barrier, owners + nc)
+        pl.semaphore_wait(barrier, owners + len(front_list))
 
     @pl.when(is_other)
     def _():
@@ -508,8 +511,14 @@
     local_or_remote(stays, side_send, side_recv.at[group], side_sems.at[0], side_sems.at[1], keeper)
     local_or_remote(stays, bulk_send, bulk_recv.at[group], bulk_sems.at[0], bulk_sems.at[1], keeper)
     from_here = host * groups + group
-    for at in range(nc):
-        to, here = device_at(0, 0, 0, at), is_front & (c == at)
+
+    @pl.when(is_other)
+    def _():
+        await_bytes(bulk_send, bulk_sems.at[0])
+
+    for x, yy, zz, cc in front_list:
+        at = cc
+        to, here = device_at(x, yy, zz, cc), is_front & (p == x) & (c == cc)
         local_or_remote(
             here, front_weight_send.at[at], front_weight.at[from_here], front_sems.at[0], front_sems.at[1], to
         )
@@ -586,15 +595,15 @@
                     block = ((at % HALVES * depth + of) * ny + at // HALVES % ny) * nc + at // (HALVES * ny)
                     block = (block * width).astype(F32)
                     wanted = [
-                        first_recv[:, :, depth + i].reshape(singles, LANES).astype(F32) + block for i in range(nc)
+                        first_recv[:, :, depth + i].reshape(singles, LANES).astype(F32) + block for i in range(blocks)
                     ]
                     wanted = mask(jnp.concatenate(wanted, axis=0) == row_key).astype(BF16)
                 if step == ITERS - 2:
                     part_send[...] = dot(wanted, flat).astype(BF16).reshape(part_send.shape)
-                    for i in range(nc):
+                    for x, yy, zz, cc in front_list:
                         remote(
-                            part_send.at[i], part_recv.at[mine], front_sems.at[4], front_sems.at[5],
-                            device_at(0, 0, 0, i),
+                            part_send.at[cc], part_recv.at[mine], front_sems.at[4], front_sems.at[5],
+                            device_at(x, yy, zz, cc),
                         )
             else:
                 for at in range(n_ka):
@@ -602,7 +611,7 @@
                     last_send[at] = terms[:, zz // depth, zz % depth, yy, cc]
 
                 def act(spot, is_here):
-                    if not sum(spot[:3]):
+                    if spot in front_list:
                         return
                     src, dst = last_send.at[(spot[2] * ny + spot[1]) * nc + spot[3]], last_recv.at[mine]
                     if is_here:
@@ -646,12 +655,13 @@
         await_bytes(first_send.at[pl.ds(0, owners - 1)], send_sem.at[0])
         for step in range(1, ITERS - 1):
             await_bytes(terms_send.at[step - 1, pl.ds(0, owners - 1)], send_sem.at[step])
-        sent = devices - nc - 1
+        sent = devices - len(front_list) - 1
         for _ in range(sent // owners):
             await_bytes(last_recv, send_sem.at[ITERS - 1])
         if sent % owners:
             await_bytes(last_recv.at[pl.ds(0, sent % owners)], send_sem.at[ITERS - 1])
-        await_bytes(part_send, front_sems.at[4])
+        for _ in range(nx):
+            await_bytes(part_send, front_sems.at[4])
 
     @pl.when(is_other)
     def _():
@@ -659,18 +669,22 @@
 
     for ref, semaphore in ((front_weight_send, front_sems.at[0]), (front_side_send, front_sems.at[2])):
 
-        @pl.when(is_front)
-        def _():
-            await_bytes(ref.at[pl.ds(0, nc - 1)], semaphore)
+        for _ in range(nx - 1):
+            await_bytes(ref, semaphore)
+
+        await_bytes(ref.at[pl.ds(0, blocks - 1)], semaphore)
 
         @pl.when(is_back)
         def _():
-            await_bytes(ref, semaphore)
+            await_bytes(ref.at[0], semaphore)
 
     @pl.when(jnp.logical_not(stays))
     def _():
         await_bytes(side_send, side_sems.at[0])
-        await_bytes(bulk_send, bulk_sems.at[0])
+
+        @pl.when(is_owner)
+        def _():
+            await_bytes(bulk_send, bulk_sems.at[0])
 
 
 def chip_grid(mesh):
@@ -696,7 +710,7 @@
     directions, bands, width = velocity.shape
     depth = nz // HALVES
     return (
-        nx * depth * tiles == LANES and nc * nx * tiles <= LANES and bands * bands == SUBLANES * LANES and (directions + 1) * bands == LANES
+        nx * depth * tiles == LANES and nx * tiles <= LANES and bands * bands == SUBLANES * LANES and (directions + 1) * bands == LANES
         and depth * width <= 256 and width == LANES
     )
 
@@ -710,6 +724,7 @@
     groups = nx * depth
     owners = nc * ny * HALVES
     singles = nx * nz * ny * nc * slots
+    blocks = nc
     operands = (
         coupling[0, 0], jnp.transpose(phonon_occ[0], (2, 0, 1)), band_window[0, 0], pair_count[0], k_target[0],
         kq_source[0], velocity.reshape(directions * bands, width), lifetime,
@@ -724,7 +739,7 @@
             pltpu.VMEM((bands // SUBLANES * coupling.shape[-1], LANES), BF16),
             pltpu.VMEM((2, tiles * SUBLANES, LANES), F32),
             pltpu.VMEM((SUBLANES * LANES, LANES), F32),
-            pltpu.VMEM((owners, depth + nc, slots, LANES), BF16),
+            pltpu.VMEM((owners, depth + blocks, slots, LANES), BF16),
             pltpu.VMEM((SUBLANES * tiles, LANES), BF16),
             pltpu.VMEM((tiles + SUBLANES, LANES), F32),
             pltpu.VMEM((groups, SUBLANES * tiles, LANES), BF16),
@@ -733,10 +748,10 @@
             pltpu.VMEM((ITERS - 2, owners, groups, depth, slots, LANES), BF16),
             pltpu.VMEM((nz * ny * nc, groups, slots, LANES), BF16),
             pltpu.VMEM((owners, groups, slots, LANES), BF16),
-            pltpu.VMEM((owners, groups, depth + nc, slots, LANES), BF16),
-            pltpu.VMEM((nc, slots * SUBLANES, LANES), BF16),
-            pltpu.VMEM((nc, 2 * slots, LANES), F32),
-            pltpu.VMEM((nc, singles, LANES), BF16),
+            pltpu.VMEM((owners, groups, depth + blocks, slots, LANES), BF16),
+            pltpu.VMEM((blocks, slots * SUBLANES, LANES), BF16),
+            pltpu.VMEM((blocks, 2 * slots, LANES), F32),
+            pltpu.VMEM((blocks, singles, LANES), BF16),
             pltpu.VMEM((owners * groups, slots * SUBLANES, LANES), BF16),
             pltpu.VMEM((owners * groups, 2 * slots, LANES), F32),
             pltpu.VMEM((owners, singles, LANES), BF16),

time: 19.6 us -> 18.9 us (0.964)
  the two profiles are of different devices: /device:TPU:3 before, /device:TPU:5 now
where the time goes in v4:
time: 18.9 us; the launch traced here: 18.8 us
  Pallas kernels  18.1 us (96%)
  local copies, waits for them, and re-layouts  0.62 us (3%)
    pallas_call x1, Pallas kernels, owner_shards(): pl.pallas_call(functools.partial(owner_kernel, grid, directions), out_sha...  18.1 us
    unnamed x1, local copies, waits for them, and re-layouts  0.62 us

profile of v4, /device:TPU:5, one launch (start us, length us, event | category | flops | bytes accessed | tf_op | source)
XLA Modules:
  0.0 18.8 jit_solution(3811584014422300472)
XLA Ops:
  0.0 18.1 %shard_map.82 = f32[96,128]{1,0:T(8,128)S(1)} custom-call(bf16[32,32,384]{2,1,0:T(8,128)(2,1)} %bitcast.11, f32[12,1,32]{2,1,0:T(1,128)} %bitcast.14, s32[32,32]{1,0:T(8,128)} %bitcast.13, s32[1,16]{1,0:T(1,128)} %bitcast.15, s32[1,32]{1,0:T(1,128)} %bitcast.16, s32[1,32]{1,0:T(1,128)} %bitcast.17, f32[96,128]{1,0:T(8,128)} %bitcast.12, f32[32,128]{1,0:T(8,128)} %refs_7_.1), custom_call_target="tpu_custom_call" | custom-call | tf_op jit(solution)/shard_map/pallas_call | solution.py:732
  18.1 0.6 %copy.10 = f32[3,32,128]{2,1,0:T(8,128)} copy(f32[3,32,128]{2,1,0:T(8,128)S(1)} %bitcast.10) | data formatting | bytes 98304

commit v5 on v4

--- a/solution.py
+++ b/solution.py
@@ -255,23 +255,9 @@
     return sorted(steps, key=lambda step: -sum(min(d, n - d) for d, n in zip(step, sizes)))
 
 
-def fold_rows(parts):
-    row = iota(parts[0].shape, 0)
-
-    def meet(a, b, width):
-        first = (row % (2 * width)) < width
-        if 2 * width == SUBLANES:
-            return jnp.where(first, a, b) + pltpu.roll(jnp.where(first, b, a), width, axis=0)
-        up = pltpu.roll(a, SUBLANES - width, axis=0)
-        down = pltpu.roll(b, width, axis=0)
-        return jnp.where(first, a, b) + jnp.where(first, up, down)
-
-    width = SUBLANES // 2
-    while width:
-        half = len(parts) // 2
-        parts = [meet(parts[j], parts[j + half], width) for j in range(half)]
-        width //= 2
-    return parts[0]
+def fold_rows(a, b):
+    first = iota(a.shape, 0) < SUBLANES // 2
+    return jnp.where(first, a, b) + pltpu.roll(jnp.where(first, b, a), SUBLANES // 2, axis=0)
 
 
 def owner_kernel(
@@ -285,8 +271,6 @@
     coupling_ref, occ_ref, window_ref, count_ref, target_ref, source_ref, velocity_ref, lifetime_ref = held
     loads = [pltpu.make_async_copy(x, y, load_sem.at[i]) for i, (x, y) in enumerate(zip(inputs[1:], held[1:]))]
     loads.append(pltpu.make_async_copy(inputs[0], coupling_ref, load_sem.at[len(loads)]))
-    for load in loads:
-        load.start()
     nx, ny, nz, nc = grid
     depth = nz // HALVES
     n_ka = nz * ny * nc
@@ -334,9 +318,10 @@
     def greet(to):
         pl.semaphore_signal(barrier, inc=1, device_id=to, device_id_type=pl.DeviceIdType.MESH)
 
-    def per_device(act):
+    def per_device(act, prepare=lambda spot: None):
         for x, yy, zz, cc in every:
             hh = zz // depth
+            prepare((x, yy, zz, cc))
             if cc == nc - 1 and zz == hh + depth - 1:
                 there = (x * ny + yy) * HALVES + hh
                 pl.when(mine == there)(functools.partial(act, (x, yy, zz, cc), True))
@@ -378,14 +363,19 @@
     def await_bytes(ref, semaphore):
         pltpu.make_async_copy(ref, ref, semaphore).wait()
 
+    for load in loads:
+        load.start()
     shape = (outer * wide, LANES)
-    chunk = iota(shape, 0) - (iota(shape, 1) % bands) * modes - (iota(shape, 1) // bands) * wide
+    def band(place):
+        return place % outer * SUBLANES + place // outer
+
+    chunk = iota(shape, 0) - band(iota(shape, 1) // outer) * modes - iota(shape, 1) % outer * wide
     gather_ref[...] = mask((chunk >= 0) & (chunk < modes)).astype(BF16)
     span = tiles * SUBLANES
     shape = (directions * LANES, LANES)
     reduce = mask(
         (iota(shape, 1) // bands == iota(shape, 0) // LANES)
-        & (iota(shape, 1) % bands // SUBLANES == iota(shape, 0) % LANES // bands)
+        & (iota(shape, 1) % outer == iota(shape, 0) % outer)
     ).astype(BF16)
 
     for load in loads[:-1]:
@@ -407,11 +397,14 @@
     long_lifetime = jnp.concatenate([lifetime] * directions, axis=0)
     source = column(source_row, eye)
     pick = mask(source == iota((tiles, width), 1).astype(F32)).astype(BF16)
-    start = (long_lifetime * velocity).astype(BF16)
-    start = jnp.concatenate(
-        [start[i * bands : (i + 1) * bands] for i in range(directions) for _ in range(outer)], axis=0
-    )
-    start = dot(pick, start, ((1,), (1,)))
+    start = (long_lifetime * velocity).astype(BF16).astype(F32)
+    first_half = iota((SUBLANES, width), 0) < outer
+    rows = []
+    for i in range(directions):
+        for place in range(0, bands, SUBLANES // outer):
+            low, high = (start[i * bands + band(at) :][:1] for at in (place, place + 1))
+            rows.append(jnp.where(first_half, low, high))
+    start = dot(pick, jnp.concatenate(rows, axis=0).astype(BF16), ((1,), (1,)))
     target = column(target_row, eye)
     in_block = iota((tiles, n_ka), 0) // slots == iota((tiles, n_ka), 1)
     live = mask((iota((tiles, 1), 0) % slots).astype(F32) < column(count_ref[...].astype(F32), in_block))
@@ -435,11 +428,11 @@
     rows_ref[1] = dot(jnp.concatenate(rows, axis=1), reduce)
 
     shown = (window_ref[...].astype(F32) * live).astype(BF16)
-    spread = mask(iota((bands, LANES), 0) == iota((bands, LANES), 1) % bands).astype(BF16)
+    spread = mask(iota((bands, LANES), 0) == band(iota((bands, LANES), 1) % bands)).astype(BF16)
     lane = iota((tiles, LANES), 1)
     terms = jnp.zeros((tiles, LANES), F32)
     for at in range(SUBLANES):
-        terms = jnp.where(lane % SUBLANES == at, rows_ref[1, pl.ds(at, tiles, stride=SUBLANES), :], terms)
+        terms = jnp.where(lane % bands // outer == at, rows_ref[1, pl.ds(at, tiles, stride=SUBLANES), :], terms)
     terms = jnp.where(lane < used, terms * dot(shown, spread), jnp.where(lane == used, target, 0.0))
     terms = terms.astype(BF16).reshape(HALVES, depth, ny, nc, slots, LANES)
     fronts = jnp.broadcast_to(source[: blocks * slots], (blocks * slots, LANES)).astype(BF16)
@@ -451,7 +444,7 @@
     copies = mask(iota((span, tiles), 0) // SUBLANES == iota((span, tiles), 1)).astype(BF16)
     shown = dot(copies, shown)
     shown = jnp.where(iota(shown.shape, 1) % SUBLANES == iota(shown.shape, 0) % SUBLANES, shown, 0.0)
-    here = mask(iota((bands, LANES), 0) // SUBLANES == iota((bands, LANES), 1) // bands)
+    here = mask(iota((bands, LANES), 0) // SUBLANES == iota((bands, LANES), 1) % outer)
     rows_ref[0] = weight * dot(shown.astype(BF16), here.astype(BF16))
     for at in range(SUBLANES):
         bulk_send[at * tiles : (at + 1) * tiles] = rows_ref[0, pl.ds(at, tiles, stride=SUBLANES), :].astype(BF16)
@@ -527,28 +520,42 @@
         )
 
     def multiply(value):
-        terms = [[] for _ in range(directions)]
-        for at in range(outer):
-            parts = [[] for _ in range(directions)]
-            for inner in range(SUBLANES):
-                totals = [None] * directions
-                for m in range(0, bands, SUBLANES):
-                    first = inner * LANES + at * bands + m
-                    factor = weight_ref[first : first + SUBLANES]
-                    for i in range(directions):
-                        term = factor * value[i * bands + m : i * bands + m + SUBLANES]
-                        totals[i] = term if totals[i] is None else totals[i] + term
+        row = iota((SUBLANES, LANES), 0) // outer
+        totals = [[None] * SUBLANES for _ in range(directions)]
+        for m in range(0, bands, SUBLANES // outer):
+            copies = []
+            for i in range(directions):
+                held_rows = value[i * bands + m // SUBLANES * SUBLANES :][:SUBLANES]
+                copies.append(jnp.take_along_axis(held_rows, row + m % SUBLANES, axis=0))
+            for at in range(SUBLANES):
+                first = at * LANES + m * outer
+                factor = weight_ref[first : first + SUBLANES]
                 for i in range(directions):
-                    parts[i].append(totals[i])
-            for i in range(directions):
-                terms[i].append(fold_rows(parts[i]))
-        return jnp.concatenate([part for found in terms for part in found], axis=0)
+                    term = factor * copies[i]
+                    totals[i][at] = term if totals[i][at] is None else totals[i][at] + term
+        return jnp.concatenate(
+            [fold_rows(*found[at : at + 2]) for found in totals for at in range(0, SUBLANES, 2)], axis=0
+        )
+
+    def reorder(rows):
+        for at in range(0, LANES, SUBLANES):
+            rows_ref[1, pl.ds(at // bands * bands + at % bands // SUBLANES, SUBLANES, stride=outer), :] = rows[
+                at : at + SUBLANES
+            ]
+        return rows_ref[1, :LANES]
+
+    def put_back(scattered):
+        rows_ref[1, :used] = scattered
+        found = [
+            rows_ref[1, pl.ds(i * bands + at, SUBLANES, stride=outer), :] for i in range(directions) for at in range(outer)
+        ]
+        return jnp.concatenate(found, axis=0)
 
     singles = devices * slots
     @pl.when(is_owner)
     def _():
         await_bytes(side_recv, side_sems.at[1])
-        both = side_recv[:, :tiles].reshape(LANES, LANES).T
+        both = reorder(side_recv[:, :tiles].reshape(LANES, LANES).T)
         velocity = both[:used]
         lifetime = jnp.concatenate([both[used:]] * directions, axis=0)
         tail = side_recv[0, tiles:]
@@ -568,7 +575,8 @@
             else:
                 await_bytes(recv.at[step - 2], recv_sem.at[step - 1])
                 arrived = recv[step - 2].reshape(LANES, LANES).T
-            value = lifetime * (velocity + dot(arrived[:used], choose))
+            found = [dot(arrived[at : at + used // 2], choose) for at in range(0, used, used // 2)]
+            value = lifetime * (velocity + jnp.concatenate(found, axis=0))
             value = value.astype(BF16).astype(F32)
             if step == 1:
                 await_bytes(bulk_recv, bulk_sems.at[1])
@@ -606,9 +614,14 @@
                             device_at(x, yy, zz, cc),
                         )
             else:
-                for at in range(n_ka):
-                    zz, yy, cc = at // (ny * nc), at // nc % ny, at % nc
-                    last_send[at] = terms[:, zz // depth, zz % depth, yy, cc]
+                stored = set()
+
+                def store(spot):
+                    yy, zz, cc = spot[1:]
+                    at = (zz * ny + yy) * nc + cc
+                    if at not in stored and spot not in front_list:
+                        stored.add(at)
+                        last_send[at] = terms[:, zz // depth, zz % depth, yy, cc]
 
                 def act(spot, is_here):
                     if spot in front_list:
@@ -619,7 +632,7 @@
                     else:
                         remote(src, dst, send_sem.at[step], recv_sem.at[step], device_at(*spot))
 
-                per_device(act)
+                per_device(act, store)
 
     @pl.when(is_front)
     def _():
@@ -630,8 +643,8 @@
         for at in range(SUBLANES):
             part = jnp.concatenate([long_rows[pl.ds(at, singles, stride=SUBLANES), :], blank], axis=0)
             weight_ref[at * LANES : (at + 1) * LANES] = part.T
-        both = front_side[:, :slots].reshape(singles, LANES)
-        scale = jnp.concatenate([both, blank], axis=0).T[used:]
+        both = reorder(jnp.concatenate([front_side[:, :slots].reshape(singles, LANES), blank], axis=0).T)
+        scale, both = both[used:], both.T[:singles]
         scale = jnp.concatenate([scale] * directions + [jnp.zeros_like(scale)], axis=0).T[:singles]
         place = front_side[:, slots:].reshape(singles, LANES) == iota((singles, width), 1).astype(F32)
         place = jnp.concatenate([mask(place), blank], axis=0).astype(BF16)
@@ -641,14 +654,14 @@
             total = total + part_recv[at].astype(F32)
         value = jnp.concatenate([scale * (both + total), blank], axis=0).astype(BF16).T.astype(F32)
         terms = dot(multiply(value[:used]).astype(BF16), place)
-        out_ref[...] = long_lifetime * (velocity + terms)
+        out_ref[...] = long_lifetime * (velocity + put_back(terms))
 
     @pl.when(is_back)
     def _():
         await_bytes(last_recv, recv_sem.at[ITERS - 1])
         arrived = last_recv[...].reshape(singles, LANES).T
         scatter = mask(arrived[used : used + 1].astype(F32) == iota((width, singles), 0).astype(F32)).astype(BF16)
-        out_ref[...] = long_lifetime * (velocity + dot(arrived[:used], scatter, ((1,), (1,))))
+        out_ref[...] = long_lifetime * (velocity + put_back(dot(arrived[:used], scatter, ((1,), (1,)))))
 
     @pl.when(is_owner)
     def _():

time: 18.9 us -> 18.9 us (level)
  no operation moved by 1% of the time
where the time goes in v5:
time: 18.9 us; the launch traced here: 18.7 us
  Pallas kernels  18 us (95%)
  local copies, waits for them, and re-layouts  0.62 us (3%)
    pallas_call x1, Pallas kernels, owner_shards(): pl.pallas_call(functools.partial(owner_kernel, grid, directions), out_sha...  18 us
    unnamed x1, local copies, waits for them, and re-layouts  0.62 us

profile of v5, /device:TPU:5, one launch (start us, length us, event | category | flops | bytes accessed | tf_op | source)
XLA Modules:
  0.0 18.7 jit_solution(8992871277583932946)
XLA Ops:
  0.0 18.0 %shard_map.82 = f32[96,128]{1,0:T(8,128)S(1)} custom-call(bf16[32,32,384]{2,1,0:T(8,128)(2,1)} %bitcast.11, f32[12,1,32]{2,1,0:T(1,128)} %bitcast.14, s32[32,32]{1,0:T(8,128)} %bitcast.13, s32[1,16]{1,0:T(1,128)} %bitcast.15, s32[1,32]{1,0:T(1,128)} %bitcast.16, s32[1,32]{1,0:T(1,128)} %bitcast.17, f32[96,128]{1,0:T(8,128)} %bitcast.12, f32[32,128]{1,0:T(8,128)} %refs_7_.1), custom_call_target="tpu_custom_call" | custom-call | tf_op jit(solution)/shard_map/pallas_call | solution.py:745
  18.1 0.6 %copy.10 = f32[3,32,128]{2,1,0:T(8,128)} copy(f32[3,32,128]{2,1,0:T(8,128)S(1)} %bitcast.10) | data formatting | bytes 98304

commit v6 on v5

--- a/solution.py
+++ b/solution.py
@@ -409,6 +409,13 @@
     in_block = iota((tiles, n_ka), 0) // slots == iota((tiles, n_ka), 1)
     live = mask((iota((tiles, 1), 0) % slots).astype(F32) < column(count_ref[...].astype(F32), in_block))
 
+    shown = (window_ref[...].astype(F32) * live).astype(BF16)
+    copies = mask(iota((span, tiles), 0) // SUBLANES == iota((span, tiles), 1)).astype(BF16)
+    long_shown = dot(copies, shown)
+    inner = iota(long_shown.shape, 1) % SUBLANES == iota(long_shown.shape, 0) % SUBLANES
+    long_shown = jnp.where(inner, long_shown, 0.0)
+    here = mask(iota((bands, LANES), 0) // SUBLANES == iota((bands, LANES), 1) % outer)
+    long_shown = dot(long_shown.astype(BF16), here.astype(BF16))
     loads[-1].wait()
     rows = [[] for _ in range(outer)]
     for tile in range(tiles):
@@ -427,7 +434,6 @@
         rows.append(jnp.concatenate(part, axis=0).astype(BF16))
     rows_ref[1] = dot(jnp.concatenate(rows, axis=1), reduce)
 
-    shown = (window_ref[...].astype(F32) * live).astype(BF16)
     spread = mask(iota((bands, LANES), 0) == band(iota((bands, LANES), 1) % bands)).astype(BF16)
     lane = iota((tiles, LANES), 1)
     terms = jnp.zeros((tiles, LANES), F32)
@@ -441,11 +447,7 @@
         first_send[(x * ny + yy) * HALVES + hh, :depth] = terms[hh, :, yy, x]
         first_send[(x * ny + yy) * HALVES + hh, depth:] = fronts
 
-    copies = mask(iota((span, tiles), 0) // SUBLANES == iota((span, tiles), 1)).astype(BF16)
-    shown = dot(copies, shown)
-    shown = jnp.where(iota(shown.shape, 1) % SUBLANES == iota(shown.shape, 0) % SUBLANES, shown, 0.0)
-    here = mask(iota((bands, LANES), 0) // SUBLANES == iota((bands, LANES), 1) % outer)
-    rows_ref[0] = weight * dot(shown.astype(BF16), here.astype(BF16))
+    rows_ref[0] = weight * long_shown
     for at in range(SUBLANES):
         bulk_send[at * tiles : (at + 1) * tiles] = rows_ref[0, pl.ds(at, tiles, stride=SUBLANES), :].astype(BF16)
 

time: 18.9 us -> 18.7 us (0.989)
  no operation moved by 1% of the time
where the time goes in v6:
time: 18.7 us; the launch traced here: 18.6 us
  Pallas kernels  17.9 us (96%)
  local copies, waits for them, and re-layouts  0.62 us (3%)
    pallas_call x1, Pallas kernels, owner_shards(): pl.pallas_call(functools.partial(owner_kernel, grid, directions), out_sha...  17.9 us
    unnamed x1, local copies, waits for them, and re-layouts  0.62 us

profile of v6, /device:TPU:5, one launch (start us, length us, event | category | flops | bytes accessed | tf_op | source)
XLA Modules:
  0.0 18.6 jit_solution(18413300653945166504)
XLA Ops:
  0.0 17.9 %shard_map.82 = f32[96,128]{1,0:T(8,128)S(1)} custom-call(bf16[32,32,384]{2,1,0:T(8,128)(2,1)} %bitcast.11, f32[12,1,32]{2,1,0:T(1,128)} %bitcast.14, s32[32,32]{1,0:T(8,128)} %bitcast.13, s32[1,16]{1,0:T(1,128)} %bitcast.15, s32[1,32]{1,0:T(1,128)} %bitcast.16, s32[1,32]{1,0:T(1,128)} %bitcast.17, f32[96,128]{1,0:T(8,128)} %bitcast.12, f32[32,128]{1,0:T(8,128)} %refs_7_.1), custom_call_target="tpu_custom_call" | custom-call | tf_op jit(solution)/shard_map/pallas_call | solution.py:747
  17.9 0.6 %copy.10 = f32[3,32,128]{2,1,0:T(8,128)} copy(f32[3,32,128]{2,1,0:T(8,128)S(1)} %bitcast.10) | data formatting | bytes 98304

commit v7 on v6

--- a/solution.py
+++ b/solution.py
@@ -451,7 +451,6 @@
     for at in range(SUBLANES):
         bulk_send[at * tiles : (at + 1) * tiles] = rows_ref[0, pl.ds(at, tiles, stride=SUBLANES), :].astype(BF16)
 
-    front_weight_send[...] = rows_ref[0, : blocks * slots * SUBLANES].astype(BF16).reshape(front_weight_send.shape)
     both = jnp.concatenate([velocity, lifetime], axis=0)
     pieces = []
     for _ in range(3):
@@ -460,10 +459,6 @@
     both = dot(pick, jnp.concatenate(pieces, axis=0), ((1,), (1,)))
     both = both[:, 2 * LANES :] + both[:, LANES : 2 * LANES] + both[:, :LANES]
     side_send[:tiles] = both
-    for at in range(blocks):
-        of = slice(at * slots, (at + 1) * slots)
-        front_side_send[at, :slots] = both[of]
-        front_side_send[at, slots:] = jnp.broadcast_to(target[of], (slots, LANES))
     shape = (SUBLANES, LANES)
     long_target = jnp.broadcast_to(jnp.concatenate([target_row] * groups, axis=1), shape)
     long_source = jnp.broadcast_to(jnp.concatenate([source_row] * groups, axis=1), shape)
@@ -506,6 +501,12 @@
     local_or_remote(stays, side_send, side_recv.at[group], side_sems.at[0], side_sems.at[1], keeper)
     local_or_remote(stays, bulk_send, bulk_recv.at[group], bulk_sems.at[0], bulk_sems.at[1], keeper)
     from_here = host * groups + group
+
+    front_weight_send[...] = rows_ref[0, : blocks * slots * SUBLANES].astype(BF16).reshape(front_weight_send.shape)
+    for at in range(blocks):
+        of = slice(at * slots, (at + 1) * slots)
+        front_side_send[at, :slots] = side_send[of]
+        front_side_send[at, slots:] = jnp.broadcast_to(target[of], (slots, LANES))
 
     @pl.when(is_other)
     def _():

time: 18.7 us -> 18.7 us (level)
  no operation moved by 1% of the time
where the time goes in v7:
time: 18.7 us; the launch traced here: 18.6 us
  Pallas kernels  17.9 us (96%)
  local copies, waits for them, and re-layouts  0.62 us (3%)
    pallas_call x1, Pallas kernels, owner_shards(): pl.pallas_call(functools.partial(owner_kernel, grid, directions), out_sha...  17.9 us
    unnamed x1, local copies, waits for them, and re-layouts  0.62 us

profile of v7, /device:TPU:5, one launch (start us, length us, event | category | flops | bytes accessed | tf_op | source)
XLA Modules:
  0.0 18.6 jit_solution(13593065238389220671)
XLA Ops:
  0.0 17.9 %shard_map.82 = f32[96,128]{1,0:T(8,128)S(1)} custom-call(bf16[32,32,384]{2,1,0:T(8,128)(2,1)} %bitcast.11, f32[12,1,32]{2,1,0:T(1,128)} %bitcast.14, s32[32,32]{1,0:T(8,128)} %bitcast.13, s32[1,16]{1,0:T(1,128)} %bitcast.15, s32[1,32]{1,0:T(1,128)} %bitcast.16, s32[1,32]{1,0:T(1,128)} %bitcast.17, f32[96,128]{1,0:T(8,128)} %bitcast.12, f32[32,128]{1,0:T(8,128)} %refs_7_.1), custom_call_target="tpu_custom_call" | custom-call | tf_op jit(solution)/shard_map/pallas_call | solution.py:748
  17.9 0.6 %copy.10 = f32[3,32,128]{2,1,0:T(8,128)} copy(f32[3,32,128]{2,1,0:T(8,128)S(1)} %bitcast.10) | data formatting | bytes 98304
